TPU v7x, 128 devices: a whole 4x4x4 slice. The times are simulated.
128 devices in a mesh: rows: 32 (over y, z, core), chan: 4 (over x).
Axes of the slice: x: 4, y: 4, z: 4, core: 2. Of those that a mesh axis runs over, the one named last changes fastest.
Arguments:
- radiances: float32 [16, 65536], P('chan', 'rows'), may hold values from -6 to 6
- band: int32 [65536, 1], P('rows'), may hold values from 0 to 31; in each aligned block of 2048 rows (0 to 2047, 2048 to 4095, ...) at most 128 rows name the same one
- row_in_band: int32 [65536], P('rows'), may hold values from 0 to 3
- column: int32 [65536], P('rows'), may hold values from 0 to 1439
Outputs:
- cell_count: int32 [128, 1440], P('rows')
- cell_mean: float32 [16, 128, 1440], P('chan', 'rows')
- cell_var: float32 [16, 128, 1440], P('chan', 'rows')
- cell_spread: float32 [128, 1440], P('rows')
- departure: float32 [16, 65536], P('chan', 'rows')
Inputs may be any that keep to these rules, and one draw needn't show every extreme that they name: Within each aligned block of 2048 observations (one scan-time shard) no band is named by more than 128 observations, and in some blocks one band is named by exactly 128.
All inputs are finite; a program needn't handle non-finite values.
Results may differ from a plain program's by a relative error of at most 0.0003.
Values sent between devices are 32-bit elements.
A program may use at most 64 MiB of HBM per device.

v0:
```python
import math

import jax
import jax.numpy as jnp
from jax import lax
from jax.sharding import PartitionSpec as P

CHAN = 16
COLS = 1440
ROWS_DEV = 4


def copy_for_each(shard, axis):
    copies = jnp.broadcast_to(shard, (lax.axis_size(axis), *shard.shape))
    return lax.all_to_all(copies, axis, split_axis=0, concat_axis=0, tiled=True)


def of_everyone(shard, axis):
    return copy_for_each(shard, axis).sum(axis=0)


def slot_ranks(dest, nrows):
    obs_dev = dest.shape[0]
    width = math.gcd(obs_dev, 128)
    nblock = obs_dev // width
    owners = jnp.arange(nrows, dtype=jnp.int32)
    hot = (dest[None, :] == owners[:, None]).astype(jnp.bfloat16).reshape(nrows, nblock, width)
    upper = (
        lax.broadcasted_iota(jnp.int32, (width, width), 0)
        <= lax.broadcasted_iota(jnp.int32, (width, width), 1)
    ).astype(jnp.bfloat16)
    inner = jnp.einsum("nbk,kj->nbj", hot, upper, preferred_element_type=jnp.float32)
    hot_float = hot.astype(jnp.float32)
    totals = jnp.sum(hot_float, axis=2)
    before = jnp.cumsum(totals, axis=1) - totals
    ranks = jnp.sum(hot_float * (inner + before[:, :, None]), axis=0).reshape(obs_dev) - 1.0
    return ranks.astype(jnp.int32)


def split_pair(values):
    high = lax.optimization_barrier(values.astype(jnp.bfloat16))
    low = (values - high.astype(jnp.float32)).astype(jnp.bfloat16)
    return (high, low)


def split_three(values):
    high = lax.optimization_barrier(values.astype(jnp.bfloat16))
    rest = values - high.astype(jnp.float32)
    middle = lax.optimization_barrier(rest.astype(jnp.bfloat16))
    low = (rest - middle.astype(jnp.float32)).astype(jnp.bfloat16)
    return (high, middle, low)


def grid_lookup(table, lat_index, col_index):
    fields, nlat, ncol = table.shape
    total = lat_index.shape[0]
    width = math.gcd(total, 2048)
    flat = table.reshape(fields * nlat, ncol)
    lat_iota = jnp.arange(nlat, dtype=jnp.int32)
    col_iota = jnp.arange(ncol, dtype=jnp.int32)

    def look_turn(turn, result):
        start = turn * width
        lat_part = lax.dynamic_slice_in_dim(lat_index, start, width, 0)
        col_part = lax.dynamic_slice_in_dim(col_index, start, width, 0)
        col_hot = (col_iota[:, None] == col_part[None, :]).astype(jnp.float32)
        picked = jnp.dot(
            flat, col_hot, precision=lax.Precision.HIGHEST, preferred_element_type=jnp.float32
        ).reshape(fields, nlat, width)
        lat_hot = (lat_iota[:, None] == lat_part[None, :]).astype(jnp.float32)
        found = jnp.sum(picked * lat_hot[None], axis=1)
        return lax.dynamic_update_slice_in_dim(result, found, start, 1)

    return lax.fori_loop(0, total // width, look_turn, jnp.zeros((fields, total), jnp.float32))


def body(radiances, band, row_in_band, column):
    nrows = lax.axis_size("rows")
    chan_dev, obs_dev = radiances.shape
    cap = 2 * obs_dev // nrows
    total_slots = nrows * cap
    dest = band[:, 0]
    slot = dest * cap + slot_ranks(dest, nrows)
    rad_high, rad_middle, rad_low = split_three(radiances)
    payload = jnp.concatenate(
        [
            rad_high,
            rad_middle,
            rad_low,
            row_in_band[None, :].astype(jnp.bfloat16),
            (column // 64)[None, :].astype(jnp.bfloat16),
            (column % 64)[None, :].astype(jnp.bfloat16),
            jnp.ones((1, obs_dev), jnp.bfloat16),
        ],
        axis=0,
    )
    nload = payload.shape[0]
    span = math.gcd(total_slots, 1024)
    slot_iota = jnp.arange(span, dtype=jnp.int32)

    def pack_turn(turn, buffer):
        start = turn * span
        hot = (slot[:, None] == (start + slot_iota)[None, :]).astype(jnp.bfloat16)
        placed_part = jnp.dot(payload, hot, preferred_element_type=jnp.float32)
        return lax.dynamic_update_slice_in_dim(buffer, placed_part, start, 1)

    placed = lax.fori_loop(
        0, total_slots // span, pack_turn, jnp.zeros((nload, total_slots), jnp.float32)
    )
    sent_values = (
        placed[0:chan_dev] + placed[chan_dev : 2 * chan_dev] + placed[2 * chan_dev : 3 * chan_dev]
    )
    base = 3 * chan_dev
    sent_cell = jnp.where(
        placed[base + 3] > 0.5,
        placed[base] * COLS + placed[base + 1] * 64.0 + placed[base + 2],
        -1.0,
    )
    packed = jnp.concatenate([sent_values, sent_cell[None, :]], axis=0).reshape(
        chan_dev + 1, nrows, cap
    )
    arrived = lax.all_to_all(packed, "rows", split_axis=1, concat_axis=1, tiled=True).reshape(
        chan_dev + 1, total_slots
    )
    values = arrived[:chan_dev]
    cell = arrived[chan_dev].astype(jnp.int32)
    lat_local = jnp.where(cell >= 0, cell // COLS, -1)
    col_local = jnp.where(cell >= 0, cell % COLS, -1)
    value_high, value_low = split_pair(values)
    square_high, square_low = split_pair(values * values)
    features = jnp.concatenate(
        [jnp.ones((1, total_slots), jnp.bfloat16), value_high, value_low, square_high, square_low],
        axis=0,
    )
    nfeat = features.shape[0]
    row_hot = (lat_local[None, :] == jnp.arange(ROWS_DEV, dtype=jnp.int32)[:, None]).astype(
        jnp.bfloat16
    )
    left = (features[:, None, :] * row_hot[None, :, :]).reshape(nfeat * ROWS_DEV, total_slots)
    block = math.gcd(total_slots, 2048)
    turns = total_slots // block
    columns_all = jnp.arange(COLS, dtype=jnp.int32)

    def accumulate(turn, acc):
        start = turn * block
        part = lax.dynamic_slice_in_dim(left, start, block, 1)
        picked = lax.dynamic_slice_in_dim(col_local, start, block, 0)
        col_hot = (picked[:, None] == columns_all[None, :]).astype(jnp.bfloat16)
        return acc + jnp.dot(part, col_hot, preferred_element_type=jnp.float32)

    sums = lax.fori_loop(0, turns, accumulate, jnp.zeros((nfeat * ROWS_DEV, COLS), jnp.float32))
    sums = sums.reshape(nfeat, ROWS_DEV, COLS)
    count = sums[0]
    first = sums[1 : 1 + chan_dev] + sums[1 + chan_dev : 1 + 2 * chan_dev]
    second = sums[1 + 2 * chan_dev : 1 + 3 * chan_dev] + sums[1 + 3 * chan_dev :]
    denom = jnp.maximum(count, 1.0)[None]
    mean = first / denom
    var = jnp.maximum(second / denom - mean * mean, 0.0)
    spread = of_everyone(jnp.sum(var, axis=0), "chan")
    scale = lax.rsqrt(1.0 + spread / CHAN)
    fields = grid_lookup(jnp.concatenate([mean, scale[None]], axis=0), lat_local, col_local)
    shifted = (values - fields[:chan_dev]) * fields[chan_dev][None, :]
    returned = lax.all_to_all(
        shifted.reshape(chan_dev, nrows, cap), "rows", split_axis=1, concat_axis=1, tiled=True
    )
    returned_flat = returned.reshape(chan_dev, total_slots)

    def unplace(turn, result):
        start = turn * span
        hot = (slot[:, None] == (start + slot_iota)[None, :]).astype(jnp.float32)
        part = lax.dynamic_slice_in_dim(returned_flat, start, span, 1)
        return result + lax.dot_general(
            part,
            hot,
            (((1,), (1,)), ((), ())),
            precision=lax.Precision.HIGHEST,
            preferred_element_type=jnp.float32,
        )

    departure = lax.fori_loop(
        0, total_slots // span, unplace, jnp.zeros((chan_dev, obs_dev), jnp.float32)
    )
    return (count.astype(jnp.int32), mean, var, spread, departure)


def solution(mesh):
    in_specs = (P("chan", "rows"), P("rows", None), P("rows"), P("rows"))
    out_specs = (
        P("rows", None),
        P("chan", "rows", None),
        P("chan", "rows", None),
        P("rows", None),
        P("chan", "rows"),
    )
    return jax.shard_map(body, mesh=mesh, in_specs=in_specs, out_specs=out_specs, check_vma=False)
```

profile of v0, /device:TPU:1, one launch (start us, length us, event | category | flops | bytes accessed | tf_op | source)
XLA Modules:
  0.0 86.2 jit_solution(15062766581898152207)
XLA Ops:
  5.1 0.8 convert_reduce_fusion
  6.1 1.0 %fusion.39 = f32[16,128]{1,0:T(8,128)S(1)} fusion(f32[32,16]{1,0:T(8,128)S(1)} %sub.41, s32[16,128]{1,0:T(8,128)} %bitcast.76), kind=kOutput, calls=%fused_computation.36 | convolution fusion | flops 17250304 | bytes 18432 | tf_op jit(solution)/shard_map/nbk,kj->nbj/dot_general | solution.py:32
  7.3 5.7 %while.56 = (s32[]{:T(128)}, f32[16,4096]{1,0:T(8,128)S(1)}, s32[2048]{0:T(1024)S(1)}, bf16[16,2048]{1,0:T(8,128)(2,1)S(1)}, s32[]{:T(128)}, /*index=5*/s32[]{:T(128)}, s32[]{:T(128)}, s32[]{:T(128)}) while((s32[]{:T(128)}, f32[16,4096]{1,0:T(8,128)S(1)}, s32[2048]{0:T(1024)S(1)}, bf16[16,2048]{1,0:T(8,128)(2,1)S(1)}, s32[]{:T(128)}, ...), condition=%wide.region_4.5_spmd.clone, body=%wide.region_3.4_spmd.clone.sunk | while | flops 69207048 | bytes 147595 | solution.py:107
  7.3 1.4 %fusion.76 = f32[16,4096]{1,0:T(8,128)S(1)} fusion(f32[16,4096]{1,0:T(8,128)S(1)} %get-tuple-element.634, s32[]{:T(128)S(6)} %select_n.106, bf16[16,2048]{1,0:T(8,128)(2,1)S(1)} %get-tuple-element.644, s32[1024]{0:T(1024)S(1)} %iota_add_fusion.4, s32[2048]{0:T(1024)S(1)} %get-tuple-element.643), kind=kOutput, calls=%fused_computation.10.clone.1 | convolution fusion | flops 69206016 | bytes 143364 | tf_op jit(solution)/shard_map/while/body/eval_jaxpr/dot_general | solution.py:104
  8.7 1.4 %fusion.76 = f32[16,4096]{1,0:T(8,128)S(1)} fusion(f32[16,4096]{1,0:T(8,128)S(1)} %get-tuple-element.634, s32[]{:T(128)S(6)} %select_n.106, bf16[16,2048]{1,0:T(8,128)(2,1)S(1)} %get-tuple-element.644, s32[1024]{0:T(1024)S(1)} %iota_add_fusion.4, s32[2048]{0:T(1024)S(1)} %get-tuple-element.643), kind=kOutput, calls=%fused_computation.10.clone.1 | convolution fusion | flops 69206016 | bytes 143364 | tf_op jit(solution)/shard_map/while/body/eval_jaxpr/dot_general | solution.py:104
  10.1 1.4 %fusion.76 = f32[16,4096]{1,0:T(8,128)S(1)} fusion(f32[16,4096]{1,0:T(8,128)S(1)} %get-tuple-element.634, s32[]{:T(128)S(6)} %select_n.106, bf16[16,2048]{1,0:T(8,128)(2,1)S(1)} %get-tuple-element.644, s32[1024]{0:T(1024)S(1)} %iota_add_fusion.4, s32[2048]{0:T(1024)S(1)} %get-tuple-element.643), kind=kOutput, calls=%fused_computation.10.clone.1 | convolution fusion | flops 69206016 | bytes 143364 | tf_op jit(solution)/shard_map/while/body/eval_jaxpr/dot_general | solution.py:104
  11.5 1.4 %fusion.76 = f32[16,4096]{1,0:T(8,128)S(1)} fusion(f32[16,4096]{1,0:T(8,128)S(1)} %get-tuple-element.634, s32[]{:T(128)S(6)} %select_n.106, bf16[16,2048]{1,0:T(8,128)(2,1)S(1)} %get-tuple-element.644, s32[1024]{0:T(1024)S(1)} %iota_add_fusion.4, s32[2048]{0:T(1024)S(1)} %get-tuple-element.643), kind=kOutput, calls=%fused_computation.10.clone.1 | convolution fusion | flops 69206016 | bytes 143364 | tf_op jit(solution)/shard_map/while/body/eval_jaxpr/dot_general | solution.py:104
  13.7 9.6 %all-to-all-start = ((f32[5,32,128]{2,0,1:T(8,128)}), f32[5,32,128]{2,0,1:T(8,128)S(1)}, u32[]{:S(2)}, u32[]{:S(2)}) async-start(f32[5,32,128]{2,0,1:T(8,128)} %pad_maximum_fusion), calls=%async_computation | async-start | bytes 262144 | tf_op jit(solution)/shard_map/all_to_all | solution.py:122
  23.3 7.7 %all-to-all-done = f32[5,32,128]{2,0,1:T(8,128)S(1)} async-done(((f32[5,32,128]{2,0,1:T(8,128)}), f32[5,32,128]{2,0,1:T(8,128)S(1)}, u32[]{:S(2)}, u32[]{:S(2)}) %all-to-all-start) | async-done | bytes 81952 | tf_op jit(solution)/shard_map/all_to_all | solution.py:122
  32.1 5.4 %while.58 = (s32[]{:T(128)}, f32[68,1440]{1,0:T(8,128)S(1)}, bf16[68,4096]{1,0:T(8,128)(2,1)S(1)}, s32[4096]{0:T(1024)S(1)}, s32[]{:T(128)}, /*index=5*/s32[]{:T(128)}, s32[]{:T(128)}, s32[]{:T(128)}) while((s32[]{:T(128)}, f32[68,1440]{1,0:T(8,128)S(1)}, bf16[68,4096]{1,0:T(8,128)(2,1)S(1)}, s32[4096]{0:T(1024)S(1)}, s32[]{:T(128)}, ...), condition=%wide.region_6.7_spmd.clone, body=%wide.region_5.6_spmd.clone.sunk | while | flops 404225280 | bytes 1153685 | solution.py:151
  32.1 2.7 %fusion.81 = f32[68,1440]{1,0:T(8,128)S(1)} fusion(s32[2048]{0:T(1024)S(1)} %dynamic_slice.52, f32[68,1440]{1,0:T(8,128)S(1)} %get-tuple-element.658, bf16[68,4096]{1,0:T(8,128)(2,1)S(1)} %get-tuple-element.667, s32[]{:T(128)S(6)} %select_n.108, pred[]{:T(512)S(6)} %compare.9), kind=kOutput, calls=%fused_computation.23.clone.1 | convolution fusion | flops 404225280 | bytes 1137157 | tf_op jit(solution)/shard_map/while/body/eval_jaxpr/dot_general | solution.py:149
  34.8 2.7 %fusion.81 = f32[68,1440]{1,0:T(8,128)S(1)} fusion(s32[2048]{0:T(1024)S(1)} %dynamic_slice.52, f32[68,1440]{1,0:T(8,128)S(1)} %get-tuple-element.658, bf16[68,4096]{1,0:T(8,128)(2,1)S(1)} %get-tuple-element.667, s32[]{:T(128)S(6)} %select_n.108, pred[]{:T(512)S(6)} %compare.9), kind=kOutput, calls=%fused_computation.23.clone.1 | convolution fusion | flops 404225280 | bytes 1137157 | tf_op jit(solution)/shard_map/while/body/eval_jaxpr/dot_general | solution.py:149
  39.6 4.0 %all-to-all-start.1 = ((f32[4,4,1440]{2,1,0:T(4,128)}), f32[4,4,1440]{2,1,0:T(4,128)S(1)}, u32[]{:S(2)}, u32[]{:S(2)}) async-start(f32[4,4,1440]{2,1,0:T(4,128)} %broadcast_in_dim.78), calls=%async_computation.1 | async-start | bytes 196608 | tf_op jit(solution)/shard_map/all_to_all | solution.py:15
  43.6 4.7 %all-to-all-done.1 = f32[4,4,1440]{2,1,0:T(4,128)S(1)} async-done(((f32[4,4,1440]{2,1,0:T(4,128)}), f32[4,4,1440]{2,1,0:T(4,128)S(1)}, u32[]{:S(2)}, u32[]{:S(2)}) %all-to-all-start.1) | async-done | bytes 92192 | tf_op jit(solution)/shard_map/all_to_all | solution.py:15
  48.9 8.0 %while.57 = (s32[]{:T(128)}, f32[5,4096]{1,0:T(8,128)S(1)}, s32[4096]{0:T(1024)S(1)}, f32[20,1440]{1,0:T(8,128)S(1)}, s32[4096]{0:T(1024)S(1)}, /*index=5*/s32[]{:T(128)}, s32[]{:T(128)}, s32[]{:T(128)}, s32[]{:T(128)}) while((s32[]{:T(128)}, f32[5,4096]{1,0:T(8,128)S(1)}, s32[4096]{0:T(1024)S(1)}, f32[20,1440]{1,0:T(8,128)S(1)}, ...), condition=%wide.region_11.12_spmd.clone, body=%wide.region_9.11_spmd.clone.sunk | while | flops 710825984 | bytes 1057431 | solution.py:74
  48.9 3.7 %fusion.78 = f32[20,2048]{1,0:T(8,128)S(1)} fusion(f32[20,1440]{1,0:T(8,128)S(1)} %get-tuple-element.694, s32[2048]{0:T(1024)S(1)} %dynamic_slice.49), kind=kOutput, calls=%fused_computation.15.clone.1 | convolution fusion | flops 710737920 | bytes 287232 | tf_op jit(solution)/shard_map/while/body/eval_jaxpr/dot_general | solution.py:67
  52.9 3.7 %fusion.78 = f32[20,2048]{1,0:T(8,128)S(1)} fusion(f32[20,1440]{1,0:T(8,128)S(1)} %get-tuple-element.694, s32[2048]{0:T(1024)S(1)} %dynamic_slice.49), kind=kOutput, calls=%fused_computation.15.clone.1 | convolution fusion | flops 710737920 | bytes 287232 | tf_op jit(solution)/shard_map/while/body/eval_jaxpr/dot_general | solution.py:67
  57.6 5.3 %all-to-all-start.2 = ((f32[4,32,128]{2,0,1:T(4,128)}), f32[4,32,128]{2,0,1:T(4,128)S(1)}, u32[]{:S(2)}, u32[]{:S(2)}) async-start(f32[4,32,128]{2,0,1:T(4,128)} %multiply_bitcast_fusion), calls=%async_computation.2 | async-start | bytes 131072 | tf_op jit(solution)/shard_map/all_to_all | solution.py:163
  62.9 7.5 %all-to-all-done.2 = f32[4,32,128]{2,0,1:T(4,128)S(1)} async-done(((f32[4,32,128]{2,0,1:T(4,128)}), f32[4,32,128]{2,0,1:T(4,128)S(1)}, u32[]{:S(2)}, u32[]{:S(2)}) %all-to-all-start.2) | async-done | bytes 65568 | tf_op jit(solution)/shard_map/all_to_all | solution.py:163
  70.3 15.2 %while.59 = (s32[]{:T(128)}, f32[4,2048]{1,0:T(4,128)S(1)}, f32[4,4096]{1,0:T(4,128)S(1)}, s32[2048]{0:T(1024)S(1)}, s32[]{:T(128)}, /*index=5*/s32[]{:T(128)}, s32[]{:T(128)}, s32[]{:T(128)}) while((s32[]{:T(128)}, f32[4,2048]{1,0:T(4,128)S(1)}, f32[4,4096]{1,0:T(4,128)S(1)}, s32[2048]{0:T(1024)S(1)}, s32[]{:T(128)}, ...), condition=%wide.region_13.14_spmd.clone, body=%wide.region_12.13_spmd.clone.sunk | while | flops 102777864 | bytes 98453 | solution.py:180
  70.3 3.8 %fusion.84 = f32[4,2048]{1,0:T(4,128)S(1)} fusion(s32[1024]{0:T(1024)S(1)} %iota_add_fusion.5, s32[2048]{0:T(1024)S(1)} %get-tuple-element.719, f32[4,2048]{1,0:T(4,128)S(1)} %get-tuple-element.709, f32[4,4096]{1,0:T(4,128)S(1)} %get-tuple-element.718, s32[]{:T(128)S(6)} %select_n.109, pred[]{:T(512)S(6)} %compare.10), kind=kOutput, calls=%fused_computation.30.clone.1 | convolution fusion | flops 102776832 | bytes 94213 | tf_op jit(solution)/shard_map/while/body/eval_jaxpr/dot_general | solution.py:172
  74.1 3.8 %fusion.84 = f32[4,2048]{1,0:T(4,128)S(1)} fusion(s32[1024]{0:T(1024)S(1)} %iota_add_fusion.5, s32[2048]{0:T(1024)S(1)} %get-tuple-element.719, f32[4,2048]{1,0:T(4,128)S(1)} %get-tuple-element.709, f32[4,4096]{1,0:T(4,128)S(1)} %get-tuple-element.718, s32[]{:T(128)S(6)} %select_n.109, pred[]{:T(512)S(6)} %compare.10), kind=kOutput, calls=%fused_computation.30.clone.1 | convolution fusion | flops 102776832 | bytes 94213 | tf_op jit(solution)/shard_map/while/body/eval_jaxpr/dot_general | solution.py:172
  77.9 3.8 %fusion.84 = f32[4,2048]{1,0:T(4,128)S(1)} fusion(s32[1024]{0:T(1024)S(1)} %iota_add_fusion.5, s32[2048]{0:T(1024)S(1)} %get-tuple-element.719, f32[4,2048]{1,0:T(4,128)S(1)} %get-tuple-element.709, f32[4,4096]{1,0:T(4,128)S(1)} %get-tuple-element.718, s32[]{:T(128)S(6)} %select_n.109, pred[]{:T(512)S(6)} %compare.10), kind=kOutput, calls=%fused_computation.30.clone.1 | convolution fusion | flops 102776832 | bytes 94213 | tf_op jit(solution)/shard_map/while/body/eval_jaxpr/dot_general | solution.py:172
  81.8 3.8 %fusion.84 = f32[4,2048]{1,0:T(4,128)S(1)} fusion(s32[1024]{0:T(1024)S(1)} %iota_add_fusion.5, s32[2048]{0:T(1024)S(1)} %get-tuple-element.719, f32[4,2048]{1,0:T(4,128)S(1)} %get-tuple-element.709, f32[4,4096]{1,0:T(4,128)S(1)} %get-tuple-element.718, s32[]{:T(128)S(6)} %select_n.109, pred[]{:T(512)S(6)} %compare.10), kind=kOutput, calls=%fused_computation.30.clone.1 | convolution fusion | flops 102776832 | bytes 94213 | tf_op jit(solution)/shard_map/while/body/eval_jaxpr/dot_general | solution.py:172
  (71 shorter events, 10.9 us)
Async XLA Ops:
  13.7 17.3 %all-to-all-start = ((f32[5,32,128]{2,0,1:T(8,128)}), f32[5,32,128]{2,0,1:T(8,128)S(1)}, u32[]{:S(2)}, u32[]{:S(2)}) async-start(f32[5,32,128]{2,0,1:T(8,128)} %pad_maximum_fusion), calls=%async_computation | async-start | bytes 262144 | tf_op jit(solution)/shard_map/all_to_all | solution.py:122
  38.9 9.5 %copy-start = (f32[4,4,1440]{2,1,0:T(4,128)}, f32[4,4,1440]{2,1,0:T(4,128)S(1)}, u32[]{:S(2)}) copy-start(f32[4,4,1440]{2,1,0:T(4,128)S(1)} %get-tuple-element.508) | copy-start | bytes 276484
  39.6 8.7 %all-to-all-start.1 = ((f32[4,4,1440]{2,1,0:T(4,128)}), f32[4,4,1440]{2,1,0:T(4,128)S(1)}, u32[]{:S(2)}, u32[]{:S(2)}) async-start(f32[4,4,1440]{2,1,0:T(4,128)} %broadcast_in_dim.78), calls=%async_computation.1 | async-start | bytes 196608 | tf_op jit(solution)/shard_map/all_to_all | solution.py:15
  48.3 0.6 copy-start.1
  57.6 12.8 %all-to-all-start.2 = ((f32[4,32,128]{2,0,1:T(4,128)}), f32[4,32,128]{2,0,1:T(4,128)S(1)}, u32[]{:S(2)}, u32[]{:S(2)}) async-start(f32[4,32,128]{2,0,1:T(4,128)} %multiply_bitcast_fusion), calls=%async_computation.2 | async-start | bytes 131072 | tf_op jit(solution)/shard_map/all_to_all | solution.py:163
  85.5 0.6 copy-start.2
where the time goes:
time: 86.9 us; the launch traced here: 86.2 us
  matrix products  34.5 us (40%)
  waiting for transfers between devices  19.8 us (23%)
  starting transfers between devices  18.9 us (22%)
  other arithmetic  8.95 us (10%)
  local copies, waits for them, and re-layouts  2.84 us (3%)
  between operations  0.92 us (1%)
    dot_general x4, matrix products, unplace(): lax.dot_general(part, hot, (((1,), (1,)), ((), ())), precision=lax.Precis...  15.1 us
    all_to_all x1, starting transfers between devices, body(): lax.all_to_all(packed, 'rows', split_axis=1, concat_axis=1, tiled=True)  9.59 us
    all_to_all x1, waiting for transfers between devices, body(): lax.all_to_all(packed, 'rows', split_axis=1, concat_axis=1, tiled=True)  7.67 us
    dot_general x2, matrix products, look_turn(): jnp.dot(flat, col_hot, precision=lax.Precision.HIGHEST, preferred_element...  7.49 us
    all_to_all x1, waiting for transfers between devices, body(): lax.all_to_all(shifted.reshape(chan_dev, nrows, cap), 'rows', split_axis=...  7.47 us
    dot_general x4, matrix products, pack_turn(): placed_part = jnp.dot(payload, hot, preferred_element_type=jnp.float32)  5.63 us
    dot_general x2, matrix products, accumulate(): return acc + jnp.dot(part, col_hot, preferred_element_type=jnp.float32)  5.3 us
    all_to_all x1, starting transfers between devices, body(): lax.all_to_all(shifted.reshape(chan_dev, nrows, cap), 'rows', split_axis=...  5.3 us
  transfers between devices with their start and end apart: 3, of which 3 were waited for; matrix products, arithmetic and copies ran while one was open for 0% of the time, Pallas kernels for 0%

commit v1 on v0

v1 whole, which is shorter than its diff:
```python
import functools

import jax
import jax.numpy as jnp
from jax import lax
from jax.experimental import pallas as pl
from jax.experimental.pallas import tpu as pltpu
from jax.sharding import PartitionSpec as P

CHAN = 16
COLS = 1440
NROW = 32
NCHAN = 4
CH = 4
OBS = 2048
CAP = 128
WIDE = 256
NCELL = 24
MESH = pl.DeviceIdType.MESH
F32 = jnp.float32
BF16 = jnp.bfloat16


def hops(offset):
    ring = (0, 1, 2, 1)
    return ring[offset >> 3] + ring[(offset >> 1) & 3]


NEAR = tuple(sorted(range(NROW), key=hops))
FAR = tuple(d for d in reversed(NEAR) if d)
GROUPS = (NEAR[:16], NEAR[16:])


def iota(shape, dim):
    return lax.broadcasted_iota(jnp.int32, shape, dim)


def rows16(row):
    return jnp.broadcast_to(row, (16, row.shape[1])).astype(BF16)


def count16(lanes):
    return iota((16, lanes), 0).astype(F32).astype(BF16)


def hot_into(ref, top, cols, names, blocks, lanes, first=0):
    one, zero = jnp.ones((16, lanes), BF16), jnp.zeros((16, lanes), BF16)
    steps = count16(lanes)
    for k in range(blocks):
        ref[top + 16 * k : top + 16 * k + 16, cols] = jnp.where(
            names == steps + jnp.asarray(16 * k + first, BF16), one, zero
        )


def high_of(x):
    return x.astype(BF16).astype(F32)


def spread_into_slots(radiances, bands, rib, column, left, right, rank_ref, tiles):
    lanes = OBS
    names = rows16(bands)
    hot_into(right, 0, slice(0, lanes), names, 2, lanes)
    blocks = [right[0:32, WIDE * j : WIDE * j + WIDE] for j in range(OBS // WIDE)]
    before, seen = [], jnp.zeros((32, WIDE), BF16)
    for block in blocks:
        before.append(seen)
        seen = seen + block
    stacked = jnp.concatenate(
        [jnp.concatenate(before, axis=0), jnp.concatenate(blocks, axis=0)], axis=1
    )
    ones = jnp.ones((WIDE, WIDE), BF16)
    upper = jnp.where(iota((WIDE, WIDE), 0) <= iota((WIDE, WIDE), 1), 1.0, 0.0).astype(BF16)
    prefix = jnp.dot(
        stacked, jnp.concatenate([ones, upper], axis=0), preferred_element_type=F32
    )
    ranks = []
    for j, block in enumerate(blocks):
        own = block.astype(F32) * prefix[32 * j : 32 * j + 32]
        ranks.append(jnp.sum(own, axis=0, keepdims=True) - 1.0)
    rank = jnp.concatenate(ranks, axis=1)
    rank_ref[...] = rank
    hot_into(right, 0, slice(0, lanes), rows16(rank), CAP // 16, lanes)

    row = iota((8, lanes), 0)
    both = jnp.concatenate([radiances, radiances], axis=0)
    high = high_of(both)
    middle = high_of(both - high)
    low = both - high - middle
    cell_hi = jnp.broadcast_to(((column >> 8) * 4 + rib + 1).astype(F32), (8, lanes))
    cell_lo = jnp.broadcast_to((column & 255).astype(F32), (8, lanes))
    names_of = jnp.where(row == 4, cell_hi, jnp.where(row == 5, cell_lo, 0.0))
    payload = jnp.concatenate(
        [jnp.where(row < 4, high, middle), jnp.where(row < 4, low, names_of)], axis=0
    ).astype(BF16)
    zero = jnp.zeros((16, lanes), BF16)
    for b in range(NROW):
        left[16 * b : 16 * b + 16, :] = jnp.where(names == jnp.asarray(b, BF16), payload, zero)
    placed = lax.dot_general(
        left[...], right[...], (((1,), (1,)), ((), ())), preferred_element_type=F32
    ).reshape(NROW, 16, CAP)
    upper_half, lower_half = placed[:, :8], placed[:, 8:]
    tile_row = iota((NROW, 8, CAP), 1)
    total = upper_half + pltpu.roll(upper_half, 4, 1) + lower_half
    tiles[...] = jnp.where(tile_row < 4, total, lower_half)


def comm_kernel(
    rad_ref,
    band_ref,
    rib_ref,
    col_ref,
    ret_ref,
    rank_ref,
    brel_ref,
    mean_ref,
    var_ref,
    count_ref,
    spread_ref,
    left,
    right,
    tiles,
    arrived,
    features,
    hot,
    sums,
    table,
    back,
    returned,
    partial,
    spreads,
    send_sem,
    recv_sem,
    ready_sem,
):
    me, mine = lax.axis_index("rows"), lax.axis_index("chan")
    peer = {d: lax.bitwise_xor(me, d) for d in range(NROW)}
    other = {k: lax.bitwise_xor(mine, k) for k in range(NCHAN)}
    barrier = pltpu.get_barrier_semaphore()
    for d in FAR:
        pl.semaphore_signal(barrier, 1, device_id={"rows": peer[d]}, device_id_type=MESH)
    for k in range(1, NCHAN):
        pl.semaphore_signal(barrier, 1, device_id={"chan": other[k]}, device_id_type=MESH)

    bands = lax.bitwise_xor(band_ref[...], me).astype(F32)
    brel_ref[...] = bands
    spread_into_slots(
        rad_ref[...], bands, rib_ref[...], col_ref[...], left, right, rank_ref, tiles
    )
    arrived[0] = tiles[0]
    pl.semaphore_wait(barrier, NROW - 1 + NCHAN - 1)

    def remote(src, dst, which, **to):
        return pltpu.make_async_remote_copy(
            src_ref=src,
            dst_ref=dst,
            send_sem=send_sem.at[which],
            recv_sem=recv_sem.at[which],
            device_id=to,
            device_id_type=MESH,
        )

    for d in FAR:
        which = 0 if d in GROUPS[0] else 1
        remote(
            tiles.at[d, pl.ds(0, 6)], arrived.at[d, pl.ds(0, 6)], which, rows=peer[d]
        ).start()
    for k in range(1, NCHAN):
        pl.semaphore_signal(ready_sem, 1, device_id={"chan": other[k]}, device_id_type=MESH)

    for g, group in enumerate(GROUPS):
        n = len(group)
        lanes = n * CAP
        cols = slice(g * lanes, (g + 1) * lanes)
        waited = arrived.at[pl.ds(0, n - (0 in group)), pl.ds(0, 6)]
        remote(waited, waited, g, rows=me).wait()
        row = iota((8, lanes), 0)
        tile = jnp.concatenate([arrived[d] for d in group], axis=1)
        value = jnp.where(row < 4, tile, pltpu.roll(tile, 4, 0))
        square = value * value
        value_hi, square_hi = high_of(value), high_of(square)
        feature = jnp.concatenate(
            [
                jnp.where(row < 4, value_hi, value - value_hi),
                jnp.where(row < 4, square_hi, square - square_hi),
            ],
            axis=0,
        ).astype(BF16)
        cell_hi = rows16(jnp.concatenate([arrived[d, 4:5] for d in group], axis=1))
        cell_lo = rows16(jnp.concatenate([arrived[d, 5:6] for d in group], axis=1))
        zero = jnp.zeros((16, lanes), BF16)
        for a in range(NCELL):
            features[16 * a : 16 * a + 16, :] = jnp.where(
                cell_hi == jnp.asarray(a + 1, BF16), feature, zero
            )
        hot_into(features, 16 * NCELL, slice(0, lanes), cell_hi, 2, lanes, first=1)
        hot_into(hot, 0, cols, cell_lo, WIDE // 16, lanes)
        part = lax.dot_general(
            features[...], hot[:, cols], (((1,), (1,)), ((), ())), preferred_element_type=F32
        )
        for half in range(2):
            piece = part[:, CAP * half : CAP * half + CAP]
            if g == 0:
                sums[half] = piece
            else:
                sums[half] += piece

    def both_halves(pick):
        return jnp.concatenate([sums[half, pick, :] for half in range(2)], axis=1)

    count = both_halves(slice(16 * NCELL, 16 * NCELL + NCELL))
    inverse = 1.0 / jnp.maximum(count, 1.0)
    means, variances = [], []
    for c in range(CH):
        pick = lambda f: both_halves(pl.ds(f, NCELL, stride=16))
        mean = (pick(c) + pick(c + 4)) * inverse
        var = jnp.maximum((pick(c + 8) + pick(c + 12)) * inverse - mean * mean, 0.0)
        means.append(mean)
        variances.append(var)
    own_spread = (variances[0] + variances[1]) + (variances[2] + variances[3])
    spreads[0] = own_spread
    fields = means + [own_spread]
    highs = [high_of(x) for x in fields]
    lows = [x - h for x, h in zip(fields, highs)]
    table[...] = jnp.concatenate(highs + lows, axis=0).astype(BF16)

    nfield = len(fields)
    order = [d for group in GROUPS for d in group]
    turn = 4
    for t in reversed(range(NROW // turn)):
        group = order[turn * t : turn * t + turn]
        lanes = turn * CAP
        found = jnp.dot(
            table[...], hot[:, lanes * t : lanes * t + lanes], preferred_element_type=F32
        ).reshape(2 * nfield, NCELL, lanes)
        found = found[:nfield] + found[nfield:]
        cell_hi = jnp.concatenate([arrived[d, 4:5] for d in group], axis=1)
        here = jnp.broadcast_to(cell_hi, (NCELL, lanes)) == (iota((NCELL, lanes), 0) + 1).astype(F32)
        row = iota((8, lanes), 0)
        looked = jnp.zeros((8, lanes), F32)
        for f in range(nfield):
            only = jnp.where(here, found[f], 0.0)
            only = only[0:8] + only[8:16] + only[16:24]
            only = only + pltpu.roll(only, 4, 0)
            only = only + pltpu.roll(only, 2, 0)
            only = only + pltpu.roll(only, 1, 0)
            looked = jnp.where(row == f, only, looked)
        tile = jnp.concatenate([arrived[d] for d in group], axis=1)
        tile = jnp.where(row < 4, tile - looked, looked)
        for i, d in enumerate(group):
            back[d] = tile[:, CAP * i : CAP * i + CAP]
        if t == NROW // turn - 1:
            pl.semaphore_wait(ready_sem, NCHAN - 1)
        for d in reversed(group):
            for k in (2, 1, 3):
                remote(
                    back.at[d, pl.ds(4, 1)],
                    partial.at[k, pl.ds(d, 1)],
                    3,
                    rows=peer[d],
                    chan=other[k],
                ).start()
            if d:
                remote(
                    back.at[d, pl.ds(0, 5)], returned.at[d, pl.ds(0, 5)], 2, rows=peer[d]
                ).start()
    for k in range(1, NCHAN):
        remote(spreads.at[0], spreads.at[k], 4, chan=other[k]).start()

    returned[0] = back[0]
    count_ref[...] = count
    for c in range(CH):
        mean_ref[c] = means[c]
        var_ref[c] = variances[c]

    waited = returned.at[pl.ds(0, NROW - 1), pl.ds(0, 5)]
    remote(waited, waited, 2, rows=me).wait()
    waited = partial.at[pl.ds(1, NCHAN - 1)]
    remote(waited, waited, 3, rows=me).wait()
    row = iota((8, CAP), 0)
    for d in range(NROW):
        rest = partial[1, d : d + 1] + partial[2, d : d + 1] + partial[3, d : d + 1]
        ret_ref[d] = returned[d] + jnp.where(row == 4, jnp.broadcast_to(rest, (8, CAP)), 0.0)
    waited = spreads.at[pl.ds(1, NCHAN - 1)]
    remote(waited, waited, 4, rows=me).wait()
    spread_ref[...] = (spreads[0] + spreads[1]) + (spreads[2] + spreads[3])


def last_kernel(
    ret_ref,
    rank_ref,
    brel_ref,
    mean_ref,
    var_ref,
    count_ref,
    spread_ref,
    count_out,
    mean_out,
    var_out,
    spread_out,
    dep_out,
    hot,
):
    for part in range(6):
        lo, hi = WIDE * part, min(WIDE * part + WIDE, COLS)
        take = (slice(4 * part, 4 * part + 4), slice(0, hi - lo))
        count_out[:, lo:hi] = count_ref[take].astype(jnp.int32)
        spread_out[:, lo:hi] = spread_ref[take]
        for c in range(CH):
            mean_out[c, :, lo:hi] = mean_ref[(c, *take)]
            var_out[c, :, lo:hi] = var_ref[(c, *take)]
    hot_into(hot, 0, slice(0, OBS), rows16(rank_ref[...]), CAP // 16, OBS)
    packed = ret_ref[...].reshape(NROW * 8, CAP)
    high = high_of(packed)
    pieces = jnp.concatenate([high, packed - high], axis=1).astype(BF16)
    lanes = 512
    for t in range(OBS // lanes):
        cols = slice(t * lanes, t * lanes + lanes)
        twice = jnp.concatenate([hot[:, cols], hot[:, cols]], axis=0)
        found = jnp.dot(pieces, twice, preferred_element_type=F32)
        names = jnp.broadcast_to(brel_ref[:, cols], (8, lanes))
        total = jnp.zeros((8, lanes), F32)
        for d in range(NROW):
            total = total + jnp.where(names == float(d), found[8 * d : 8 * d + 8], 0.0)
        scale = lax.rsqrt(1.0 + total[4:5] / CHAN)
        dep_out[:, cols] = total[0:4] * scale


def body(radiances, band, row_in_band, column):
    vmem = pl.BlockSpec(memory_space=pltpu.VMEM)
    shape = jax.ShapeDtypeStruct
    grid = (NCELL, WIDE)
    made = pl.pallas_call(
        comm_kernel,
        out_shape=(
            shape((NROW, 8, CAP), F32),
            shape((1, OBS), F32),
            shape((1, OBS), F32),
            shape((CH, *grid), F32),
            shape((CH, *grid), F32),
            shape(grid, F32),
            shape(grid, F32),
        ),
        in_specs=[vmem] * 4,
        out_specs=(vmem,) * 7,
        scratch_shapes=[
            pltpu.VMEM((16 * NROW, OBS), BF16),
            pltpu.VMEM((CAP, OBS), BF16),
            pltpu.VMEM((NROW, 8, CAP), F32),
            pltpu.VMEM((NROW, 8, CAP), F32),
            pltpu.VMEM((16 * NCELL + 32, 16 * CAP), BF16),
            pltpu.VMEM((WIDE, NROW * CAP), BF16),
            pltpu.VMEM((2, 16 * NCELL + 32, CAP), F32),
            pltpu.VMEM((10 * NCELL, WIDE), BF16),
            pltpu.VMEM((NROW, 8, CAP), F32),
            pltpu.VMEM((NROW, 8, CAP), F32),
            pltpu.VMEM((NCHAN, NROW, CAP), F32),
            pltpu.VMEM((NCHAN, *grid), F32),
            pltpu.SemaphoreType.DMA((5,)),
            pltpu.SemaphoreType.DMA((5,)),
            pltpu.SemaphoreType.REGULAR,
        ],
        compiler_params=pltpu.CompilerParams(collective_id=0, has_side_effects=True),
    )(
        radiances,
        band.reshape(1, OBS),
        row_in_band.reshape(1, OBS),
        column.reshape(1, OBS),
    )
    return pl.pallas_call(
        last_kernel,
        out_shape=(
            shape((4, COLS), jnp.int32),
            shape((CH, 4, COLS), F32),
            shape((CH, 4, COLS), F32),
            shape((4, COLS), F32),
            shape((CH, OBS), F32),
        ),
        in_specs=[vmem] * 7,
        out_specs=(vmem,) * 5,
        scratch_shapes=[pltpu.VMEM((CAP, OBS), BF16)],
    )(*made)


def solution(mesh):
    in_specs = (P("chan", "rows"), P("rows", None), P("rows"), P("rows"))
    out_specs = (
        P("rows", None),
        P("chan", "rows", None),
        P("chan", "rows", None),
        P("rows", None),
        P("chan", "rows"),
    )
    return jax.shard_map(body, mesh=mesh, in_specs=in_specs, out_specs=out_specs, check_vma=False)
```

time: 86.9 us -> 25.4 us (0.29)
  matrix products: 34.5 us -> 0 us
  Pallas kernels: 0 us -> 24.6 us
  waiting for transfers between devices: 19.8 us -> 0 us
  starting transfers between devices: 18.9 us -> 0 us
  other arithmetic: 8.95 us -> 0 us
  local copies, waits for them, and re-layouts: 2.84 us -> 0 us
    dot_general x13 -> x0, matrix products: 34.5 us -> none  [the longest x4 15.1 us: unplace(): lax.dot_general(part, hot, (((1,), (1,)), ((), ())), precision=lax.Precis...]
    pallas_call x0 -> x2, Pallas kernels: none -> 24.6 us  [the longest x1 22.5 us: body(): pl.pallas_call(comm_kernel, out_shape=(shape((NROW, 8, CAP), F32), shape(...]
    all_to_all x3 -> x0, waiting for transfers between devices: 19.8 us -> none  [the longest x1 7.67 us: body(): lax.all_to_all(packed, 'rows', split_axis=1, concat_axis=1, tiled=True)]
    all_to_all x3 -> x0, starting transfers between devices: 18.9 us -> none  [the longest x1 9.59 us: body(): lax.all_to_all(packed, 'rows', split_axis=1, concat_axis=1, tiled=True)]
    convert_element_type x10 -> x0, other arithmetic: 3.81 us -> none  [the longest x1 0.78 us: split_three(): low = (rest - middle.astype(jnp.float32)).astype(jnp.bfloat16)]
    reduce_sum x5 -> x0, other arithmetic: 1.78 us -> none  [the longest x1 0.83 us: slot_ranks(): totals = jnp.sum(hot_float, axis=2)]
    unnamed x6 -> x0, local copies, waits for them, and re-layouts: 1.09 us -> none
    mul x2 -> x0, other arithmetic: 1 us -> none  [the longest x1 0.71 us: body(): slot = dest * cap + slot_ranks(dest, nrows)]
  transfers between devices with their start and end apart: 3 -> 0, of which waited for: 3 -> 0; matrix products, arithmetic and copies ran while one was open for 0% -> 0% of each run, Pallas kernels for 0% -> 0%
where the time goes in v1:
time: 25.4 us; the launch traced here: 25.2 us
  Pallas kernels  24.6 us (97%)
  between operations  0.64 us (3%)
    pallas_call x1, Pallas kernels, body(): pl.pallas_call(comm_kernel, out_shape=(shape((NROW, 8, CAP), F32), shape(...  22.5 us
    pallas_call x1, Pallas kernels, body(): pl.pallas_call(last_kernel, out_shape=(shape((4, COLS), jnp.int32), shape...  2.16 us

profile of v1, /device:TPU:1, one launch (start us, length us, event | category | flops | bytes accessed | tf_op | source)
XLA Modules:
  0.0 25.2 jit_solution(14261475464036188945)
XLA Ops:
  0.6 22.5 %shard_map.83 = (f32[32,8,128]{2,1,0:T(8,128)}, f32[1,2048]{1,0:T(1,128)}, f32[1,2048]{1,0:T(1,128)}, f32[4,24,256]{2,1,0:T(8,128)}, f32[4,24,256]{2,1,0:T(8,128...) custom-call(f32[4,2048]{1,0:T(4,128)} %rad_ref.1, s32[1,2048]{1,0:T(1,128)} %bitcast.3, s32[1,2048]{1,0:T(1,128)} %bitcast.4, ...), custom_call_target="tpu_custom_call" | custom-call | tf_op jit(solution)/shard_map/pallas_call | solution.py:332
  23.1 2.2 %shard_map.84 = (s32[4,1440]{1,0:T(4,128)}, f32[4,4,1440]{2,1,0:T(4,128)}, f32[4,4,1440]{2,1,0:T(4,128)}, f32[4,1440]{1,0:T(4,128)}, f32[4,2048]{1,0:T(4,128)}) custom-call(f32[32,8,128]{2,1,0:T(8,128)} %get-tuple-element.12.ret_ref, f32[1,2048]{1,0:T(1,128)} %get-tuple-element.13.rank_ref, f32[1,2048]{1,0:T(1,128)} %get-tuple-element.14.brel_ref, ...), custom_call_target="tpu_custom_call" | custom-call | tf_op jit(solution)/shard_map/pallas_call | solution.py:369

commit v2 on v1

--- a/solution.py
+++ b/solution.py
@@ -105,10 +105,10 @@
 
 
 def comm_kernel(
-    rad_ref,
-    band_ref,
-    rib_ref,
-    col_ref,
+    rad_hbm,
+    band_hbm,
+    rib_hbm,
+    col_hbm,
     ret_ref,
     rank_ref,
     brel_ref,
@@ -116,6 +116,10 @@
     var_ref,
     count_ref,
     spread_ref,
+    rad_ref,
+    band_ref,
+    rib_ref,
+    col_ref,
     left,
     right,
     tiles,
@@ -131,7 +135,16 @@
     send_sem,
     recv_sem,
     ready_sem,
+    load_sem,
 ):
+    loads = [
+        pltpu.make_async_copy(src, dst, load_sem.at[i])
+        for i, (src, dst) in enumerate(
+            ((band_hbm, band_ref), (rad_hbm, rad_ref), (rib_hbm, rib_ref), (col_hbm, col_ref))
+        )
+    ]
+    for load in loads:
+        load.start()
     me, mine = lax.axis_index("rows"), lax.axis_index("chan")
     peer = {d: lax.bitwise_xor(me, d) for d in range(NROW)}
     other = {k: lax.bitwise_xor(mine, k) for k in range(NCHAN)}
@@ -141,6 +154,8 @@
     for k in range(1, NCHAN):
         pl.semaphore_signal(barrier, 1, device_id={"chan": other[k]}, device_id_type=MESH)
 
+    for load in loads:
+        load.wait()
     bands = lax.bitwise_xor(band_ref[...], me).astype(F32)
     brel_ref[...] = bands
     spread_into_slots(
@@ -340,9 +355,13 @@
             shape(grid, F32),
             shape(grid, F32),
         ),
-        in_specs=[vmem] * 4,
+        in_specs=[pl.BlockSpec(memory_space=pltpu.HBM)] * 4,
         out_specs=(vmem,) * 7,
         scratch_shapes=[
+            pltpu.VMEM((CH, OBS), F32),
+            pltpu.VMEM((1, OBS), jnp.int32),
+            pltpu.VMEM((1, OBS), jnp.int32),
+            pltpu.VMEM((1, OBS), jnp.int32),
             pltpu.VMEM((16 * NROW, OBS), BF16),
             pltpu.VMEM((CAP, OBS), BF16),
             pltpu.VMEM((NROW, 8, CAP), F32),
@@ -358,13 +377,21 @@
             pltpu.SemaphoreType.DMA((5,)),
             pltpu.SemaphoreType.DMA((5,)),
             pltpu.SemaphoreType.REGULAR,
+            pltpu.SemaphoreType.DMA((4,)),
         ],
-        compiler_params=pltpu.CompilerParams(collective_id=0, has_side_effects=True),
+        compiler_params=pltpu.CompilerParams(
+            collective_id=0, has_side_effects=True, vmem_limit_bytes=24 << 20
+        ),
     )(
-        radiances,
-        band.reshape(1, OBS),
-        row_in_band.reshape(1, OBS),
-        column.reshape(1, OBS),
+        *(
+            pltpu.with_memory_space_constraint(x, pltpu.HBM)
+            for x in (
+                radiances,
+                band.reshape(1, OBS),
+                row_in_band.reshape(1, OBS),
+                column.reshape(1, OBS),
+            )
+        )
     )
     return pl.pallas_call(
         last_kernel,
@@ -378,6 +405,7 @@
         in_specs=[vmem] * 7,
         out_specs=(vmem,) * 5,
         scratch_shapes=[pltpu.VMEM((CAP, OBS), BF16)],
+        compiler_params=pltpu.CompilerParams(vmem_limit_bytes=16 << 20),
     )(*made)
 
 

time: 25.4 us -> 22.9 us (0.902)
  Pallas kernels: 24.6 us -> 22.1 us
    pallas_call x1, Pallas kernels: 22.5 us -> 21 us  [body(): pl.pallas_call(comm_kernel, out_shape=(shape((NROW, 8, CAP), F32), shape(...]
    pallas_call x1, Pallas kernels: 2.16 us -> 1.1 us  [body(): pl.pallas_call(last_kernel, out_shape=(shape((4, COLS), jnp.int32), shape...]
where the time goes in v2:
time: 22.9 us; the launch traced here: 22.7 us
  Pallas kernels  22.1 us (97%)
  between operations  0.64 us (3%)
    pallas_call x1, Pallas kernels, body(): pl.pallas_call(comm_kernel, out_shape=(shape((NROW, 8, CAP), F32), shape(...  21 us
    pallas_call x1, Pallas kernels, body(): pl.pallas_call(last_kernel, out_shape=(shape((4, COLS), jnp.int32), shape...  1.1 us

profile of v2, /device:TPU:1, one launch (start us, length us, event | category | flops | bytes accessed | tf_op | source)
XLA Modules:
  0.0 22.7 jit_solution(12972850147085515256)
XLA Ops:
  0.6 21.0 %shard_map.83 = (f32[32,8,128]{2,1,0:T(8,128)S(1)}, f32[1,2048]{1,0:T(1,128)S(1)}, f32[1,2048]{1,0:T(1,128)S(1)}, f32[4,24,256]{2,1,0:T(8,128)S(1)}, f32[4,24,25...) custom-call(f32[4,2048]{1,0:T(4,128)} %rad_hbm.1, s32[1,2048]{1,0:T(1,128)} %bitcast.3, ...), custom_call_target="tpu_custom_call" | custom-call | tf_op jit(solution)/shard_map/pallas_call | solution.py:347
  21.6 1.1 %shard_map.84 = (s32[4,1440]{1,0:T(4,128)}, f32[4,4,1440]{2,1,0:T(4,128)}, f32[4,4,1440]{2,1,0:T(4,128)}, f32[4,1440]{1,0:T(4,128)}, f32[4,2048]{1,0:T(4,128)}) custom-call(f32[32,8,128]{2,1,0:T(8,128)S(1)} %get-tuple-element.12.ret_ref, f32[1,2048]{1,0:T(1,128)S(1)} %get-tuple-element.13.rank_ref, f32[1,2048]{1,0:T(1,128)S(1)} %get-tuple-element.14.brel_ref, ...), custom_call_target="tpu_custom_call" | custom-call | tf_op jit(solution)/shard_map/pallas_call | solution.py:396

commit v3 on v2

v3 whole, which is shorter than its diff:
```python
import functools

import jax
import jax.numpy as jnp
from jax import lax
from jax.experimental import pallas as pl
from jax.experimental.pallas import tpu as pltpu
from jax.sharding import PartitionSpec as P

CHAN = 16
COLS = 1440
NROW = 32
NCHAN = 4
CH = 4
OBS = 2048
CAP = 128
WIDE = 256
NCELL = 24
MESH = pl.DeviceIdType.MESH
F32 = jnp.float32
BF16 = jnp.bfloat16


def hops(offset):
    ring = (0, 1, 2, 1)
    return ring[offset >> 3] + ring[(offset >> 1) & 3]


NEAR = tuple(sorted(range(NROW), key=hops))
FAR = tuple(d for d in reversed(NEAR) if d)
GROUPS = (NEAR[0:8], NEAR[8:20], NEAR[20:32])
BACK = (NEAR,)
FIELDS = 16


def iota(shape, dim):
    return lax.broadcasted_iota(jnp.int32, shape, dim)


def rows16(row):
    return jnp.broadcast_to(row, (16, row.shape[1])).astype(BF16)


def count16(lanes):
    return iota((16, lanes), 0).astype(F32).astype(BF16)


def hot_into(ref, top, cols, names, blocks, lanes, first=0):
    one, zero = jnp.ones((16, lanes), BF16), jnp.zeros((16, lanes), BF16)
    steps = count16(lanes)
    for k in range(blocks):
        ref[top + 16 * k : top + 16 * k + 16, cols] = jnp.where(
            names == steps + jnp.asarray(16 * k + first, BF16), one, zero
        )


def high_of(x):
    return x.astype(BF16).astype(F32)


def spread_into_slots(radiances, bands, rib, column, left, right, tiles):
    lanes = OBS
    names = rows16(bands)
    hot_into(right, 0, slice(0, lanes), names, 2, lanes)
    blocks = [right[0:32, WIDE * j : WIDE * j + WIDE] for j in range(OBS // WIDE)]
    before, seen = [], jnp.zeros((32, WIDE), BF16)
    for block in blocks:
        before.append(seen)
        seen = seen + block
    stacked = jnp.concatenate(
        [jnp.concatenate(before, axis=0), jnp.concatenate(blocks, axis=0)], axis=1
    )
    ones = jnp.ones((WIDE, WIDE), BF16)
    upper = jnp.where(iota((WIDE, WIDE), 0) <= iota((WIDE, WIDE), 1), 1.0, 0.0).astype(BF16)
    prefix = jnp.dot(
        stacked, jnp.concatenate([ones, upper], axis=0), preferred_element_type=F32
    )
    ranks = []
    for j, block in enumerate(blocks):
        own = block.astype(F32) * prefix[32 * j : 32 * j + 32]
        ranks.append(jnp.sum(own, axis=0, keepdims=True) - 1.0)
    rank = jnp.concatenate(ranks, axis=1)
    hot_into(right, 0, slice(0, lanes), rows16(rank), CAP // 16, lanes)

    row = iota((8, lanes), 0)
    both = jnp.concatenate([radiances, radiances], axis=0)
    high = high_of(both)
    middle = high_of(both - high)
    low = both - high - middle
    cell_hi = jnp.broadcast_to(((column >> 8) * 4 + rib + 1).astype(F32), (8, lanes))
    cell_lo = jnp.broadcast_to((column & 255).astype(F32), (8, lanes))
    names_of = jnp.where(row == 4, cell_hi, jnp.where(row == 5, cell_lo, 0.0))
    payload = jnp.concatenate(
        [jnp.where(row < 4, high, middle), jnp.where(row < 4, low, names_of)], axis=0
    ).astype(BF16)
    zero = jnp.zeros((16, lanes), BF16)
    for b in range(NROW):
        left[16 * b : 16 * b + 16, 0:OBS] = jnp.where(names == jnp.asarray(b, BF16), payload, zero)
    placed = lax.dot_general(
        left[:, 0:OBS], right[...], (((1,), (1,)), ((), ())), preferred_element_type=F32
    ).reshape(NROW, 16, CAP)
    upper_half, lower_half = placed[:, :8], placed[:, 8:]
    tile_row = iota((NROW, 8, CAP), 1)
    total = upper_half + pltpu.roll(upper_half, 4, 1) + lower_half
    tiles[...] = jnp.where(
        tile_row < 4, total, lower_half * 256.0 + pltpu.roll(lower_half, 7, 1)
    )


def feature_rows(ref, f1, f2, lanes):
    first = jnp.broadcast_to(ref[f1 : f1 + 1, 0:lanes], (8, lanes))
    second = jnp.broadcast_to(ref[f2 : f2 + 1, 0:lanes], (8, lanes))
    return [
        jnp.concatenate(pair, axis=0).astype(BF16)
        for pair in ((first, first), (first, second), (second, second))
    ]


def accumulate(arrived, group, rows, left, hot, cols):
    lanes = len(group) * CAP
    row = iota((8, lanes), 0)
    tile = jnp.concatenate([arrived[d] for d in group], axis=1)
    code = jnp.concatenate(
        [jnp.broadcast_to(arrived[d, 4:5], (8, CAP)) for d in group], axis=1
    )
    value = jnp.where(row < 4, tile, pltpu.roll(tile, 4, 0))
    square = value * value
    value_hi, square_hi = high_of(value), high_of(square)
    rows[0:8, 0:lanes] = jnp.where(row < 4, value_hi, value - value_hi)
    rows[8:16, 0:lanes] = jnp.where(row < 4, square_hi, square - square_hi)
    cell_hi = jnp.floor(code * (1.0 / 256.0))
    cell_lo = code - 256.0 * cell_hi
    hi16 = jnp.concatenate([cell_hi, cell_hi], axis=0).astype(BF16)
    lo16 = jnp.concatenate([cell_lo, cell_lo], axis=0).astype(BF16)
    step = iota((16, lanes), 0)
    names = (step + 1, jnp.where(step < 8, step + 17, step - 7), step + 9)
    masks = [hi16 == n.astype(F32).astype(BF16) for n in names]
    zero = jnp.zeros((16, lanes), BF16)
    for pair in range(FIELDS // 2):
        for i, source in enumerate(feature_rows(rows, 2 * pair, 2 * pair + 1, lanes)):
            at = 48 * pair + 16 * i
            left[at : at + 16, 0:lanes] = jnp.where(masks[i], source, zero)
    hot_into(left, FIELDS * NCELL, slice(0, lanes), hi16, 2, lanes, first=1)
    hot_into(hot, 0, cols, lo16, WIDE // 16, lanes)
    return lax.dot_general(
        left[0 : FIELDS * NCELL + 32, 0:lanes],
        hot[:, cols],
        (((1,), (1,)), ((), ())),
        preferred_element_type=F32,
    )


def comm_kernel(
    rad_hbm,
    band_hbm,
    rib_hbm,
    col_hbm,
    count_out,
    mean_out,
    var_out,
    spread_out,
    ret_ref,
    right,
    brel,
    rad_ref,
    band_ref,
    rib_ref,
    col_ref,
    left,
    tiles,
    arrived,
    rows,
    hot,
    sums,
    table,
    back,
    returned,
    partial,
    spreads,
    send_sem,
    recv_sem,
    ready_sem,
    load_sem,
):
    loads = [
        pltpu.make_async_copy(src, dst, load_sem.at[i])
        for i, (src, dst) in enumerate(
            ((band_hbm, band_ref), (rad_hbm, rad_ref), (rib_hbm, rib_ref), (col_hbm, col_ref))
        )
    ]
    for load in loads:
        load.start()
    me, mine = lax.axis_index("rows"), lax.axis_index("chan")
    peer = {d: lax.bitwise_xor(me, d) for d in range(NROW)}
    other = {k: lax.bitwise_xor(mine, k) for k in range(NCHAN)}
    barrier = pltpu.get_barrier_semaphore()
    for d in FAR:
        pl.semaphore_signal(barrier, 1, device_id={"rows": peer[d]}, device_id_type=MESH)
    for k in range(1, NCHAN):
        pl.semaphore_signal(barrier, 1, device_id={"chan": other[k]}, device_id_type=MESH)

    for load in loads:
        load.wait()
    bands = lax.bitwise_xor(band_ref[...], me).astype(F32)
    brel[...] = bands
    spread_into_slots(rad_ref[...], bands, rib_ref[...], col_ref[...], left, right, tiles)
    arrived[0] = tiles[0]
    pl.semaphore_wait(barrier, NROW - 1 + NCHAN - 1)

    def remote(src, dst, which, **to):
        return pltpu.make_async_remote_copy(
            src_ref=src,
            dst_ref=dst,
            send_sem=send_sem.at[which],
            recv_sem=recv_sem.at[which],
            device_id=to,
            device_id_type=MESH,
        )

    def group_of(d, groups):
        return [d in group for group in groups].index(True)

    def wait_tiles(buffer, group, which):
        part = buffer.at[pl.ds(0, len(group) - (0 in group)), pl.ds(0, 5)]
        remote(part, part, which, rows=me).wait()

    first_back = len(GROUPS)
    first_part = first_back + len(BACK)
    grid_sem = first_part + len(BACK)

    for d in FAR:
        remote(
            tiles.at[d, pl.ds(0, 5)],
            arrived.at[d, pl.ds(0, 5)],
            group_of(d, GROUPS),
            rows=peer[d],
        ).start()
    for k in range(1, NCHAN):
        pl.semaphore_signal(ready_sem, 1, device_id={"chan": other[k]}, device_id_type=MESH)

    start = 0
    for g, group in enumerate(GROUPS):
        if len(group) > (0 in group):
            wait_tiles(arrived, group, g)
        cols = slice(start, start + len(group) * CAP)
        part = accumulate(arrived, group, rows, left, hot, cols)
        start = cols.stop
        if g == 0:
            sums[...] = part
        elif g < len(GROUPS) - 1:
            sums[...] += part

    def field(f):
        at = slice(NCELL * f, NCELL * f + NCELL)
        return part[at] + sums[at]

    count = field(FIELDS)
    inverse = 1.0 / jnp.maximum(count, 1.0)
    means, variances = [], []
    for c in range(CH):
        mean = (field(c) + field(c + 4)) * inverse
        var = jnp.maximum((field(c + 8) + field(c + 12)) * inverse - mean * mean, 0.0)
        means.append(mean)
        variances.append(var)
    own_spread = (variances[0] + variances[1]) + (variances[2] + variances[3])
    spreads[0] = own_spread
    fields = means + [own_spread]
    highs = [high_of(x) for x in fields]
    lows = [x - h for x, h in zip(fields, highs)]
    table[...] = jnp.concatenate(highs + lows, axis=0).astype(BF16)

    nfield = len(fields)
    order = [d for group in GROUPS for d in group]
    turn = 4
    for t in reversed(range(NROW // turn)):
        group = order[turn * t : turn * t + turn]
        lanes = turn * CAP
        looks = jnp.dot(
            table[...], hot[:, lanes * t : lanes * t + lanes], preferred_element_type=F32
        ).reshape(2 * nfield, NCELL, lanes)
        looks = looks[:nfield] + looks[nfield:]
        code = jnp.concatenate(
            [jnp.broadcast_to(arrived[d, 4:5], (8, CAP)) for d in group], axis=1
        )
        cell_hi = jnp.floor(code * (1.0 / 256.0))
        row = iota((8, lanes), 0)
        here = [cell_hi == (row + (8 * i + 1)).astype(F32) for i in range(NCELL // 8)]
        looked = jnp.zeros((8, lanes), F32)
        for f in range(nfield):
            only = jnp.where(here[0], looks[f, 0:8], 0.0)
            for i in range(1, NCELL // 8):
                only = only + jnp.where(here[i], looks[f, 8 * i : 8 * i + 8], 0.0)
            only = only + pltpu.roll(only, 4, 0)
            only = only + pltpu.roll(only, 2, 0)
            only = only + pltpu.roll(only, 1, 0)
            looked = jnp.where(row == f, only, looked)
        tile = jnp.concatenate([arrived[d] for d in group], axis=1)
        tile = jnp.where(row < 4, tile - looked, looked)
        for i, d in enumerate(group):
            back[d] = tile[:, CAP * i : CAP * i + CAP]
        if t == NROW // turn - 1:
            pl.semaphore_wait(ready_sem, NCHAN - 1)
        for d in reversed(group):
            g = group_of(d, BACK)
            for k in (2, 1, 3):
                remote(
                    back.at[d, pl.ds(4, 1)],
                    partial.at[pl.ds((k - 1) * NROW + d, 1)],
                    first_part + g,
                    rows=peer[d],
                    chan=other[k],
                ).start()
            if d:
                remote(
                    back.at[d, pl.ds(0, 5)],
                    returned.at[d, pl.ds(0, 5)],
                    first_back + g,
                    rows=peer[d],
                ).start()

    for k in range(1, NCHAN):
        remote(spreads.at[0], spreads.at[k], grid_sem, chan=other[k]).start()

    def to_rows(part, out, grid):
        lo, hi = WIDE * part, min(WIDE * part + WIDE, COLS)
        out[:, lo:hi] = grid[4 * part : 4 * part + 4, 0 : hi - lo].astype(out.dtype)

    returned[0] = back[0]
    for part in range(6):
        to_rows(part, count_out, count)
        for c in range(CH):
            to_rows(part, mean_out.at[c], means[c])
            to_rows(part, var_out.at[c], variances[c])

    wait_tiles(returned, NEAR, first_back)
    waited = spreads.at[pl.ds(1, NCHAN - 1)]
    remote(waited, waited, grid_sem, rows=me).wait()
    spread = (spreads[0] + spreads[1]) + (spreads[2] + spreads[3])
    for part in range(6):
        to_rows(part, spread_out, spread)
    remote(partial, partial, first_part, rows=me).wait()
    row = iota((8, CAP), 0)
    for d in range(NROW):
        at = [slice(k * NROW + d, k * NROW + d + 1) for k in range(NCHAN - 1)]
        rest = partial[at[0]] + partial[at[1]] + partial[at[2]]
        ret_ref[d] = returned[d] + jnp.where(row == 4, jnp.broadcast_to(rest, (8, CAP)), 0.0)


def last_kernel(
    count_ref,
    mean_ref,
    var_ref,
    spread_ref,
    ret_ref,
    right,
    brel,
    count_hbm,
    mean_hbm,
    var_hbm,
    spread_hbm,
    dep_hbm,
    dep_ref,
    sem,
):
    pairs = (
        (mean_ref, mean_hbm),
        (var_ref, var_hbm),
        (count_ref, count_hbm),
        (spread_ref, spread_hbm),
        (dep_ref, dep_hbm),
    )
    copies = [
        pltpu.make_async_copy(src, dst, sem.at[i]) for i, (src, dst) in enumerate(pairs)
    ]
    for copy in copies[:4]:
        copy.start()
    packed = ret_ref[...].reshape(NROW * 8, CAP)
    high = high_of(packed)
    pieces = jnp.concatenate([high, packed - high], axis=1).astype(BF16)
    lanes = 512
    for t in range(OBS // lanes):
        cols = slice(t * lanes, t * lanes + lanes)
        twice = jnp.concatenate([right[:, cols], right[:, cols]], axis=0)
        found = jnp.dot(pieces, twice, preferred_element_type=F32)
        names = jnp.broadcast_to(brel[:, cols], (8, lanes))
        total = jnp.zeros((8, lanes), F32)
        for d in range(NROW):
            total = total + jnp.where(names == float(d), found[8 * d : 8 * d + 8], 0.0)
        dep_ref[:, cols] = total[0:4] * lax.rsqrt(1.0 + total[4:5] / CHAN)
    copies[4].start()
    for copy in copies:
        copy.wait()


def body(radiances, band, row_in_band, column):
    vmem = pl.BlockSpec(memory_space=pltpu.VMEM)
    hbm = pl.BlockSpec(memory_space=pltpu.HBM)
    shape = jax.ShapeDtypeStruct
    grid = (NCELL, WIDE)
    outs = (
        shape((4, COLS), jnp.int32),
        shape((CH, 4, COLS), F32),
        shape((CH, 4, COLS), F32),
        shape((4, COLS), F32),
        shape((CH, OBS), F32),
    )
    between = (
        *outs[:4],
        shape((NROW, 8, CAP), F32),
        shape((CAP, OBS), BF16),
        shape((1, OBS), F32),
    )
    nsem = len(GROUPS) + 2 * len(BACK) + 1
    operands = (
        radiances,
        band.reshape(1, OBS),
        row_in_band.reshape(1, OBS),
        column.reshape(1, OBS),
    )
    made = pl.pallas_call(
        comm_kernel,
        out_shape=between,
        in_specs=[hbm] * 4,
        out_specs=(vmem,) * 7,
        scratch_shapes=[
            pltpu.VMEM((CH, OBS), F32),
            pltpu.VMEM((1, OBS), jnp.int32),
            pltpu.VMEM((1, OBS), jnp.int32),
            pltpu.VMEM((1, OBS), jnp.int32),
            pltpu.VMEM((16 * NROW, 22 * CAP), BF16),
            pltpu.VMEM((NROW, 8, CAP), F32),
            pltpu.VMEM((NROW, 8, CAP), F32),
            pltpu.VMEM((FIELDS, 22 * CAP), F32),
            pltpu.VMEM((WIDE, NROW * CAP), BF16),
            pltpu.VMEM((FIELDS * NCELL + 32, WIDE), F32),
            pltpu.VMEM((10 * NCELL, WIDE), BF16),
            pltpu.VMEM((NROW, 8, CAP), F32),
            pltpu.VMEM((NROW, 8, CAP), F32),
            pltpu.VMEM(((NCHAN - 1) * NROW, CAP), F32),
            pltpu.VMEM((NCHAN, *grid), F32),
            pltpu.SemaphoreType.DMA((nsem,)),
            pltpu.SemaphoreType.DMA((nsem,)),
            pltpu.SemaphoreType.REGULAR,
            pltpu.SemaphoreType.DMA((4,)),
        ],
        compiler_params=pltpu.CompilerParams(
            collective_id=0, has_side_effects=True, vmem_limit_bytes=24 << 20
        ),
    )(*(pltpu.with_memory_space_constraint(x, pltpu.HBM) for x in operands))
    return pl.pallas_call(
        last_kernel,
        out_shape=outs,
        in_specs=[vmem] * 7,
        out_specs=(hbm,) * 5,
        scratch_shapes=[pltpu.VMEM((CH, OBS), F32), pltpu.SemaphoreType.DMA((5,))],
        compiler_params=pltpu.CompilerParams(vmem_limit_bytes=16 << 20),
    )(*made)


def solution(mesh):
    in_specs = (P("chan", "rows"), P("rows", None), P("rows"), P("rows"))
    out_specs = (
        P("rows", None),
        P("chan", "rows", None),
        P("chan", "rows", None),
        P("rows", None),
        P("chan", "rows"),
    )
    return jax.shard_map(body, mesh=mesh, in_specs=in_specs, out_specs=out_specs, check_vma=False)
```

time: 22.9 us -> 22.7 us (level)
    pallas_call x2, Pallas kernels: 22.1 us -> 21.9 us  [the longest x1 20.7 us: body(): pl.pallas_call(comm_kernel, out_shape=between, in_specs=[hbm] * 4, out_sp...]
where the time goes in v3:
time: 22.7 us; the launch traced here: 22.5 us
  Pallas kernels  21.9 us (96%)
  between operations  0.64 us (3%)
    pallas_call x1, Pallas kernels, body(): pl.pallas_call(comm_kernel, out_shape=between, in_specs=[hbm] * 4, out_sp...  20.7 us
    pallas_call x1, Pallas kernels, body(): pl.pallas_call(last_kernel, out_shape=outs, in_specs=[vmem] * 7, out_spec...  1.12 us

profile of v3, /device:TPU:1, one launch (start us, length us, event | category | flops | bytes accessed | tf_op | source)
XLA Modules:
  0.0 22.5 jit_solution(6556514748560758168)
XLA Ops:
  0.6 20.7 %shard_map.83 = (s32[4,1440]{1,0:T(4,128)S(1)}, f32[4,4,1440]{2,1,0:T(4,128)S(1)}, f32[4,4,1440]{2,1,0:T(4,128)S(1)}, f32[4,1440]{1,0:T(4,128)S(1)}, f32[32,8,12...) custom-call(f32[4,2048]{1,0:T(4,128)} %rad_hbm.1, s32[1,2048]{1,0:T(1,128)} %bitcast.3, ...), custom_call_target="tpu_custom_call" | custom-call | tf_op jit(solution)/shard_map/pallas_call | solution.py:420
  21.4 1.1 %shard_map.84 = (s32[4,1440]{1,0:T(4,128)}, f32[4,4,1440]{2,1,0:T(4,128)}, f32[4,4,1440]{2,1,0:T(4,128)}, f32[4,1440]{1,0:T(4,128)}, f32[4,2048]{1,0:T(4,128)}) custom-call(s32[4,1440]{1,0:T(4,128)S(1)} %get-tuple-element.12.count_ref, f32[4,4,1440]{2,1,0:T(4,128)S(1)} %get-tuple-element.13.mean_ref, f32[4,4,1440]{2,1,0:T(4,128)S(1)} %get-tuple-element.14.var_ref, ...), custom_call_target="tpu_custom_call" | custom-call | tf_op jit(solution)/shard_map/pallas_call | solution.py:450

commit v4 on v3

--- a/solution.py
+++ b/solution.py
@@ -58,7 +58,7 @@
     return x.astype(BF16).astype(F32)
 
 
-def spread_into_slots(radiances, bands, rib, column, left, right, tiles):
+def spread_into_slots(radiances, bands, rib, column, left, right, rank_ref, tiles):
     lanes = OBS
     names = rows16(bands)
     hot_into(right, 0, slice(0, lanes), names, 2, lanes)
@@ -80,6 +80,7 @@
         own = block.astype(F32) * prefix[32 * j : 32 * j + 32]
         ranks.append(jnp.sum(own, axis=0, keepdims=True) - 1.0)
     rank = jnp.concatenate(ranks, axis=1)
+    rank_ref[...] = rank
     hot_into(right, 0, slice(0, lanes), rows16(rank), CAP // 16, lanes)
 
     row = iota((8, lanes), 0)
@@ -95,9 +96,9 @@
     ).astype(BF16)
     zero = jnp.zeros((16, lanes), BF16)
     for b in range(NROW):
-        left[16 * b : 16 * b + 16, 0:OBS] = jnp.where(names == jnp.asarray(b, BF16), payload, zero)
+        left[16 * b : 16 * b + 16, :] = jnp.where(names == jnp.asarray(b, BF16), payload, zero)
     placed = lax.dot_general(
-        left[:, 0:OBS], right[...], (((1,), (1,)), ((), ())), preferred_element_type=F32
+        left[...], right[...], (((1,), (1,)), ((), ())), preferred_element_type=F32
     ).reshape(NROW, 16, CAP)
     upper_half, lower_half = placed[:, :8], placed[:, 8:]
     tile_row = iota((NROW, 8, CAP), 1)
@@ -159,14 +160,16 @@
     mean_out,
     var_out,
     spread_out,
-    ret_ref,
-    right,
+    shifted_ref,
+    slots_ref,
+    rank_ref,
     brel,
     rad_ref,
     band_ref,
     rib_ref,
     col_ref,
     left,
+    right,
     tiles,
     arrived,
     rows,
@@ -203,7 +206,9 @@
         load.wait()
     bands = lax.bitwise_xor(band_ref[...], me).astype(F32)
     brel[...] = bands
-    spread_into_slots(rad_ref[...], bands, rib_ref[...], col_ref[...], left, right, tiles)
+    spread_into_slots(
+        rad_ref[...], bands, rib_ref[...], col_ref[...], left, right, rank_ref, tiles
+    )
     arrived[0] = tiles[0]
     pl.semaphore_wait(barrier, NROW - 1 + NCHAN - 1)
 
@@ -268,6 +273,20 @@
     highs = [high_of(x) for x in fields]
     lows = [x - h for x, h in zip(fields, highs)]
     table[...] = jnp.concatenate(highs + lows, axis=0).astype(BF16)
+
+    def send_partial(d, k):
+        remote(
+            back.at[d, pl.ds(4, 1)],
+            partial.at[pl.ds((k - 1) * NROW + d, 1)],
+            first_part,
+            rows=peer[d],
+            chan=other[k],
+        ).start()
+
+    def send_back(d):
+        remote(
+            back.at[d, pl.ds(0, 5)], returned.at[d, pl.ds(0, 5)], first_back, rows=peer[d]
+        ).start()
 
     nfield = len(fields)
     order = [d for group in GROUPS for d in group]
@@ -300,24 +319,11 @@
             back[d] = tile[:, CAP * i : CAP * i + CAP]
         if t == NROW // turn - 1:
             pl.semaphore_wait(ready_sem, NCHAN - 1)
-        for d in reversed(group):
-            g = group_of(d, BACK)
-            for k in (2, 1, 3):
-                remote(
-                    back.at[d, pl.ds(4, 1)],
-                    partial.at[pl.ds((k - 1) * NROW + d, 1)],
-                    first_part + g,
-                    rows=peer[d],
-                    chan=other[k],
-                ).start()
-            if d:
-                remote(
-                    back.at[d, pl.ds(0, 5)],
-                    returned.at[d, pl.ds(0, 5)],
-                    first_back + g,
-                    rows=peer[d],
-                ).start()
-
+        for k in (2, 1, 3):
+            for d in reversed(group):
+                send_partial(d, k)
+    for d in FAR:
+        send_back(d)
     for k in range(1, NCHAN):
         remote(spreads.at[0], spreads.at[k], grid_sem, chan=other[k]).start()
 
@@ -333,17 +339,29 @@
             to_rows(part, var_out.at[c], variances[c])
 
     wait_tiles(returned, NEAR, first_back)
+    packed = returned[...].reshape(NROW * 8, CAP)
+    high = high_of(packed)
+    pieces = jnp.concatenate([high, packed - high], axis=1).astype(BF16)
+    lanes = 512
+    for t in range(OBS // lanes):
+        cols = slice(t * lanes, t * lanes + lanes)
+        twice = jnp.concatenate([right[:, cols], right[:, cols]], axis=0)
+        found = jnp.dot(pieces, twice, preferred_element_type=F32)
+        names = jnp.broadcast_to(brel[:, cols], (8, lanes))
+        total = jnp.zeros((8, lanes), F32)
+        for d in range(NROW):
+            total = total + jnp.where(names == float(d), found[8 * d : 8 * d + 8], 0.0)
+        shifted_ref[:, cols] = total[0:4]
+    for d in range(NROW):
+        slots_ref[d : d + 1] = returned[d, 4:5]
     waited = spreads.at[pl.ds(1, NCHAN - 1)]
     remote(waited, waited, grid_sem, rows=me).wait()
     spread = (spreads[0] + spreads[1]) + (spreads[2] + spreads[3])
     for part in range(6):
         to_rows(part, spread_out, spread)
     remote(partial, partial, first_part, rows=me).wait()
-    row = iota((8, CAP), 0)
-    for d in range(NROW):
-        at = [slice(k * NROW + d, k * NROW + d + 1) for k in range(NCHAN - 1)]
-        rest = partial[at[0]] + partial[at[1]] + partial[at[2]]
-        ret_ref[d] = returned[d] + jnp.where(row == 4, jnp.broadcast_to(rest, (8, CAP)), 0.0)
+    rest = (partial[0:NROW] + partial[NROW : 2 * NROW]) + partial[2 * NROW :]
+    slots_ref[...] += rest
 
 
 def last_kernel(
@@ -351,8 +369,9 @@
     mean_ref,
     var_ref,
     spread_ref,
-    ret_ref,
-    right,
+    shifted_ref,
+    slots_ref,
+    rank_ref,
     brel,
     count_hbm,
     mean_hbm,
@@ -374,19 +393,20 @@
     ]
     for copy in copies[:4]:
         copy.start()
-    packed = ret_ref[...].reshape(NROW * 8, CAP)
-    high = high_of(packed)
-    pieces = jnp.concatenate([high, packed - high], axis=1).astype(BF16)
-    lanes = 512
-    for t in range(OBS // lanes):
-        cols = slice(t * lanes, t * lanes + lanes)
-        twice = jnp.concatenate([right[:, cols], right[:, cols]], axis=0)
-        found = jnp.dot(pieces, twice, preferred_element_type=F32)
-        names = jnp.broadcast_to(brel[:, cols], (8, lanes))
-        total = jnp.zeros((8, lanes), F32)
-        for d in range(NROW):
-            total = total + jnp.where(names == float(d), found[8 * d : 8 * d + 8], 0.0)
-        dep_ref[:, cols] = total[0:4] * lax.rsqrt(1.0 + total[4:5] / CHAN)
+    table = [slots_ref[8 * i : 8 * i + 8] for i in range(NROW // 8)]
+    row = iota((8, CAP), 0)
+    for t in range(OBS // CAP):
+        cols = slice(t * CAP, t * CAP + CAP)
+        at = jnp.broadcast_to(rank_ref[:, cols], (8, CAP)).astype(jnp.int32)
+        names = jnp.broadcast_to(brel[:, cols], (8, CAP)).astype(jnp.int32)
+        spread = jnp.zeros((8, CAP), F32)
+        for i, lines in enumerate(table):
+            there = jnp.take_along_axis(lines, at, axis=1, mode="promise_in_bounds")
+            spread = spread + jnp.where(names == row + 8 * i, there, 0.0)
+        spread = spread + pltpu.roll(spread, 4, 0)
+        spread = spread + pltpu.roll(spread, 2, 0)
+        spread = spread + pltpu.roll(spread, 1, 0)
+        dep_ref[:, cols] = shifted_ref[:, cols] * lax.rsqrt(1.0 + spread[0:4] / CHAN)
     copies[4].start()
     for copy in copies:
         copy.wait()
@@ -406,8 +426,9 @@
     )
     between = (
         *outs[:4],
-        shape((NROW, 8, CAP), F32),
-        shape((CAP, OBS), BF16),
+        shape((CH, OBS), F32),
+        shape((NROW, CAP), F32),
+        shape((1, OBS), F32),
         shape((1, OBS), F32),
     )
     nsem = len(GROUPS) + 2 * len(BACK) + 1
@@ -421,13 +442,14 @@
         comm_kernel,
         out_shape=between,
         in_specs=[hbm] * 4,
-        out_specs=(vmem,) * 7,
+        out_specs=(vmem,) * 8,
         scratch_shapes=[
             pltpu.VMEM((CH, OBS), F32),
             pltpu.VMEM((1, OBS), jnp.int32),
             pltpu.VMEM((1, OBS), jnp.int32),
             pltpu.VMEM((1, OBS), jnp.int32),
-            pltpu.VMEM((16 * NROW, 22 * CAP), BF16),
+            pltpu.VMEM((16 * NROW, OBS), BF16),
+            pltpu.VMEM((CAP, OBS), BF16),
             pltpu.VMEM((NROW, 8, CAP), F32),
             pltpu.VMEM((NROW, 8, CAP), F32),
             pltpu.VMEM((FIELDS, 22 * CAP), F32),
@@ -450,7 +472,7 @@
     return pl.pallas_call(
         last_kernel,
         out_shape=outs,
-        in_specs=[vmem] * 7,
+        in_specs=[vmem] * 8,
         out_specs=(hbm,) * 5,
         scratch_shapes=[pltpu.VMEM((CH, OBS), F32), pltpu.SemaphoreType.DMA((5,))],
         compiler_params=pltpu.CompilerParams(vmem_limit_bytes=16 << 20),

time: 22.7 us -> 22.4 us (0.987)
  Pallas kernels: 21.9 us -> 21.6 us
    pallas_call x1, Pallas kernels: 1.12 us -> 0.88 us  [body(): pl.pallas_call(last_kernel, out_shape=outs, in_specs=[vmem] * 8, out_spec...]
where the time goes in v4:
time: 22.4 us; the launch traced here: 22.2 us
  Pallas kernels  21.6 us (96%)
  between operations  0.64 us (3%)
    pallas_call x1, Pallas kernels, body(): pl.pallas_call(comm_kernel, out_shape=between, in_specs=[hbm] * 4, out_sp...  20.7 us
    pallas_call x1, Pallas kernels, body(): pl.pallas_call(last_kernel, out_shape=outs, in_specs=[vmem] * 8, out_spec...  0.88 us

profile of v4, /device:TPU:1, one launch (start us, length us, event | category | flops | bytes accessed | tf_op | source)
XLA Modules:
  0.0 22.2 jit_solution(842588327779400717)
XLA Ops:
  0.6 20.7 %shard_map.83 = (s32[4,1440]{1,0:T(4,128)S(1)}, f32[4,4,1440]{2,1,0:T(4,128)S(1)}, f32[4,4,1440]{2,1,0:T(4,128)S(1)}, f32[4,1440]{1,0:T(4,128)S(1)}, f32[4,2048]...) custom-call(f32[4,2048]{1,0:T(4,128)} %rad_hbm.1, s32[1,2048]{1,0:T(1,128)} %bitcast.3, ...), custom_call_target="tpu_custom_call" | custom-call | tf_op jit(solution)/shard_map/pallas_call | solution.py:441
  21.3 0.9 %shard_map.84 = (s32[4,1440]{1,0:T(4,128)}, f32[4,4,1440]{2,1,0:T(4,128)}, f32[4,4,1440]{2,1,0:T(4,128)}, f32[4,1440]{1,0:T(4,128)}, f32[4,2048]{1,0:T(4,128)}) custom-call(s32[4,1440]{1,0:T(4,128)S(1)} %get-tuple-element.13.count_ref, f32[4,4,1440]{2,1,0:T(4,128)S(1)} %get-tuple-element.14.mean_ref, f32[4,4,1440]{2,1,0:T(4,128)S(1)} %get-tuple-element.15.var_ref, ...), custom_call_target="tpu_custom_call" | custom-call | tf_op jit(solution)/shard_map/pallas_call | solution.py:472

commit v5 on v4

--- a/solution.py
+++ b/solution.py
@@ -28,7 +28,7 @@
 
 NEAR = tuple(sorted(range(NROW), key=hops))
 FAR = tuple(d for d in reversed(NEAR) if d)
-GROUPS = (NEAR[0:8], NEAR[8:20], NEAR[20:32])
+GROUPS = (NEAR[0:8], NEAR[8:20], NEAR[20:28], NEAR[28:32])
 BACK = (NEAR,)
 FIELDS = 16
 

time: 22.4 us -> 22.3 us (level)
  no operation moved by 1% of the time
where the time goes in v5:
time: 22.3 us; the launch traced here: 22.1 us
  Pallas kernels  21.4 us (96%)
  between operations  0.64 us (3%)
    pallas_call x1, Pallas kernels, body(): pl.pallas_call(comm_kernel, out_shape=between, in_specs=[hbm] * 4, out_sp...  20.6 us
    pallas_call x1, Pallas kernels, body(): pl.pallas_call(last_kernel, out_shape=outs, in_specs=[vmem] * 8, out_spec...  0.88 us

profile of v5, /device:TPU:1, one launch (start us, length us, event | category | flops | bytes accessed | tf_op | source)
XLA Modules:
  0.0 22.1 jit_solution(7364878057226480001)
XLA Ops:
  0.6 20.6 %shard_map.83 = (s32[4,1440]{1,0:T(4,128)S(1)}, f32[4,4,1440]{2,1,0:T(4,128)S(1)}, f32[4,4,1440]{2,1,0:T(4,128)S(1)}, f32[4,1440]{1,0:T(4,128)S(1)}, f32[4,2048]...) custom-call(f32[4,2048]{1,0:T(4,128)} %rad_hbm.1, s32[1,2048]{1,0:T(1,128)} %bitcast.3, ...), custom_call_target="tpu_custom_call" | custom-call | tf_op jit(solution)/shard_map/pallas_call | solution.py:441
  21.2 0.9 %shard_map.84 = (s32[4,1440]{1,0:T(4,128)}, f32[4,4,1440]{2,1,0:T(4,128)}, f32[4,4,1440]{2,1,0:T(4,128)}, f32[4,1440]{1,0:T(4,128)}, f32[4,2048]{1,0:T(4,128)}) custom-call(s32[4,1440]{1,0:T(4,128)S(1)} %get-tuple-element.13.count_ref, f32[4,4,1440]{2,1,0:T(4,128)S(1)} %get-tuple-element.14.mean_ref, f32[4,4,1440]{2,1,0:T(4,128)S(1)} %get-tuple-element.15.var_ref, ...), custom_call_target="tpu_custom_call" | custom-call | tf_op jit(solution)/shard_map/pallas_call | solution.py:472

commit v6 on v5

--- a/solution.py
+++ b/solution.py
@@ -176,6 +176,7 @@
     hot,
     sums,
     table,
+    own,
     back,
     returned,
     partial,
@@ -272,11 +273,13 @@
     fields = means + [own_spread]
     highs = [high_of(x) for x in fields]
     lows = [x - h for x, h in zip(fields, highs)]
-    table[...] = jnp.concatenate(highs + lows, axis=0).astype(BF16)
+    table[...] = jnp.concatenate(
+        [highs[CH], lows[CH], *highs[:CH], *lows[:CH]], axis=0
+    ).astype(BF16)
 
     def send_partial(d, k):
         remote(
-            back.at[d, pl.ds(4, 1)],
+            own.at[pl.ds(d, 1)],
             partial.at[pl.ds((k - 1) * NROW + d, 1)],
             first_part,
             rows=peer[d],
@@ -288,14 +291,12 @@
             back.at[d, pl.ds(0, 5)], returned.at[d, pl.ds(0, 5)], first_back, rows=peer[d]
         ).start()
 
-    nfield = len(fields)
     order = [d for group in GROUPS for d in group]
-    turn = 4
-    for t in reversed(range(NROW // turn)):
-        group = order[turn * t : turn * t + turn]
-        lanes = turn * CAP
+
+    def look(lines, group, t, nfield):
+        lanes = len(group) * CAP
         looks = jnp.dot(
-            table[...], hot[:, lanes * t : lanes * t + lanes], preferred_element_type=F32
+            table[lines, :], hot[:, lanes * t : lanes * t + lanes], preferred_element_type=F32
         ).reshape(2 * nfield, NCELL, lanes)
         looks = looks[:nfield] + looks[nfield:]
         code = jnp.concatenate(
@@ -304,26 +305,44 @@
         cell_hi = jnp.floor(code * (1.0 / 256.0))
         row = iota((8, lanes), 0)
         here = [cell_hi == (row + (8 * i + 1)).astype(F32) for i in range(NCELL // 8)]
-        looked = jnp.zeros((8, lanes), F32)
+        result = []
         for f in range(nfield):
             only = jnp.where(here[0], looks[f, 0:8], 0.0)
             for i in range(1, NCELL // 8):
                 only = only + jnp.where(here[i], looks[f, 8 * i : 8 * i + 8], 0.0)
             only = only + pltpu.roll(only, 4, 0)
             only = only + pltpu.roll(only, 2, 0)
-            only = only + pltpu.roll(only, 1, 0)
-            looked = jnp.where(row == f, only, looked)
-        tile = jnp.concatenate([arrived[d] for d in group], axis=1)
-        tile = jnp.where(row < 4, tile - looked, looked)
+            result.append(only + pltpu.roll(only, 1, 0))
+        return result
+
+    turn = 8
+    for t in reversed(range(NROW // turn)):
+        group = order[turn * t : turn * t + turn]
+        (looked,) = look(slice(0, 2 * NCELL), group, t, 1)
         for i, d in enumerate(group):
-            back[d] = tile[:, CAP * i : CAP * i + CAP]
+            own[d : d + 1] = looked[0:1, CAP * i : CAP * i + CAP]
         if t == NROW // turn - 1:
             pl.semaphore_wait(ready_sem, NCHAN - 1)
         for k in (2, 1, 3):
             for d in reversed(group):
                 send_partial(d, k)
-    for d in FAR:
-        send_back(d)
+
+    turn = 8
+    for t in reversed(range(NROW // turn)):
+        group = order[turn * t : turn * t + turn]
+        row = iota((8, turn * CAP), 0)
+        looked = jnp.concatenate(
+            [jnp.broadcast_to(own[d : d + 1], (8, CAP)) for d in group], axis=1
+        )
+        for f, mean in enumerate(look(slice(2 * NCELL, None), group, t, CH)):
+            looked = jnp.where(row == f, mean, looked)
+        tile = jnp.concatenate([arrived[d] for d in group], axis=1)
+        tile = jnp.where(row < 4, tile - looked, looked)
+        for i, d in enumerate(group):
+            back[d] = tile[:, CAP * i : CAP * i + CAP]
+        for d in reversed(group):
+            if d:
+                send_back(d)
     for k in range(1, NCHAN):
         remote(spreads.at[0], spreads.at[k], grid_sem, chan=other[k]).start()
 
@@ -456,6 +475,7 @@
             pltpu.VMEM((WIDE, NROW * CAP), BF16),
             pltpu.VMEM((FIELDS * NCELL + 32, WIDE), F32),
             pltpu.VMEM((10 * NCELL, WIDE), BF16),
+            pltpu.VMEM((NROW, CAP), F32),
             pltpu.VMEM((NROW, 8, CAP), F32),
             pltpu.VMEM((NROW, 8, CAP), F32),
             pltpu.VMEM(((NCHAN - 1) * NROW, CAP), F32),

time: 22.3 us -> 22.1 us (level)
  no operation moved by 1% of the time
where the time goes in v6:
time: 22.1 us; the launch traced here: 21.9 us
  Pallas kernels  21.2 us (96%)
  between operations  0.64 us (3%)
    pallas_call x1, Pallas kernels, body(): pl.pallas_call(comm_kernel, out_shape=between, in_specs=[hbm] * 4, out_sp...  20.4 us
    pallas_call x1, Pallas kernels, body(): pl.pallas_call(last_kernel, out_shape=outs, in_specs=[vmem] * 8, out_spec...  0.88 us

profile of v6, /device:TPU:1, one launch (start us, length us, event | category | flops | bytes accessed | tf_op | source)
XLA Modules:
  0.0 21.9 jit_solution(16747266075659469477)
XLA Ops:
  0.6 20.4 %shard_map.83 = (s32[4,1440]{1,0:T(4,128)S(1)}, f32[4,4,1440]{2,1,0:T(4,128)S(1)}, f32[4,4,1440]{2,1,0:T(4,128)S(1)}, f32[4,1440]{1,0:T(4,128)S(1)}, f32[4,2048]...) custom-call(f32[4,2048]{1,0:T(4,128)} %rad_hbm.1, s32[1,2048]{1,0:T(1,128)} %bitcast.3, ...), custom_call_target="tpu_custom_call" | custom-call | tf_op jit(solution)/shard_map/pallas_call | solution.py:460
  21.0 0.9 %shard_map.84 = (s32[4,1440]{1,0:T(4,128)}, f32[4,4,1440]{2,1,0:T(4,128)}, f32[4,4,1440]{2,1,0:T(4,128)}, f32[4,1440]{1,0:T(4,128)}, f32[4,2048]{1,0:T(4,128)}) custom-call(s32[4,1440]{1,0:T(4,128)S(1)} %get-tuple-element.13.count_ref, f32[4,4,1440]{2,1,0:T(4,128)S(1)} %get-tuple-element.14.mean_ref, f32[4,4,1440]{2,1,0:T(4,128)S(1)} %get-tuple-element.15.var_ref, ...), custom_call_target="tpu_custom_call" | custom-call | tf_op jit(solution)/shard_map/pallas_call | solution.py:492

commit v7 on v6

--- a/solution.py
+++ b/solution.py
@@ -115,6 +115,12 @@
         jnp.concatenate(pair, axis=0).astype(BF16)
         for pair in ((first, first), (first, second), (second, second))
     ]
+
+
+def hi_and_lo(fields):
+    highs = [high_of(x) for x in fields]
+    lows = [x - h for x, h in zip(fields, highs)]
+    return jnp.concatenate(highs + lows, axis=0).astype(BF16)
 
 
 def accumulate(arrived, group, rows, left, hot, cols):
@@ -176,6 +182,7 @@
     hot,
     sums,
     table,
+    spread_table,
     own,
     back,
     returned,
@@ -270,12 +277,7 @@
         variances.append(var)
     own_spread = (variances[0] + variances[1]) + (variances[2] + variances[3])
     spreads[0] = own_spread
-    fields = means + [own_spread]
-    highs = [high_of(x) for x in fields]
-    lows = [x - h for x, h in zip(fields, highs)]
-    table[...] = jnp.concatenate(
-        [highs[CH], lows[CH], *highs[:CH], *lows[:CH]], axis=0
-    ).astype(BF16)
+    spread_table[...] = hi_and_lo([own_spread])
 
     def send_partial(d, k):
         remote(
@@ -293,10 +295,10 @@
 
     order = [d for group in GROUPS for d in group]
 
-    def look(lines, group, t, nfield):
+    def look(table, group, t, nfield):
         lanes = len(group) * CAP
         looks = jnp.dot(
-            table[lines, :], hot[:, lanes * t : lanes * t + lanes], preferred_element_type=F32
+            table[...], hot[:, lanes * t : lanes * t + lanes], preferred_element_type=F32
         ).reshape(2 * nfield, NCELL, lanes)
         looks = looks[:nfield] + looks[nfield:]
         code = jnp.concatenate(
@@ -318,7 +320,7 @@
     turn = 8
     for t in reversed(range(NROW // turn)):
         group = order[turn * t : turn * t + turn]
-        (looked,) = look(slice(0, 2 * NCELL), group, t, 1)
+        (looked,) = look(spread_table, group, t, 1)
         for i, d in enumerate(group):
             own[d : d + 1] = looked[0:1, CAP * i : CAP * i + CAP]
         if t == NROW // turn - 1:
@@ -327,6 +329,7 @@
             for d in reversed(group):
                 send_partial(d, k)
 
+    table[...] = hi_and_lo(means)
     turn = 8
     for t in reversed(range(NROW // turn)):
         group = order[turn * t : turn * t + turn]
@@ -334,7 +337,7 @@
         looked = jnp.concatenate(
             [jnp.broadcast_to(own[d : d + 1], (8, CAP)) for d in group], axis=1
         )
-        for f, mean in enumerate(look(slice(2 * NCELL, None), group, t, CH)):
+        for f, mean in enumerate(look(table, group, t, CH)):
             looked = jnp.where(row == f, mean, looked)
         tile = jnp.concatenate([arrived[d] for d in group], axis=1)
         tile = jnp.where(row < 4, tile - looked, looked)
@@ -474,7 +477,8 @@
             pltpu.VMEM((FIELDS, 22 * CAP), F32),
             pltpu.VMEM((WIDE, NROW * CAP), BF16),
             pltpu.VMEM((FIELDS * NCELL + 32, WIDE), F32),
-            pltpu.VMEM((10 * NCELL, WIDE), BF16),
+            pltpu.VMEM((8 * NCELL, WIDE), BF16),
+            pltpu.VMEM((2 * NCELL, WIDE), BF16),
             pltpu.VMEM((NROW, CAP), F32),
             pltpu.VMEM((NROW, 8, CAP), F32),
             pltpu.VMEM((NROW, 8, CAP), F32),

time: 22.1 us -> 22.1 us (level)
  no operation moved by 1% of the time
where the time goes in v7:
time: 22.1 us; the launch traced here: 21.9 us
  Pallas kernels  21.2 us (96%)
  between operations  0.64 us (3%)
    pallas_call x1, Pallas kernels, body(): pl.pallas_call(comm_kernel, out_shape=between, in_specs=[hbm] * 4, out_sp...  20.4 us
    pallas_call x1, Pallas kernels, body(): pl.pallas_call(last_kernel, out_shape=outs, in_specs=[vmem] * 8, out_spec...  0.88 us

profile of v7, /device:TPU:1, one launch (start us, length us, event | category | flops | bytes accessed | tf_op | source)
XLA Modules:
  0.0 21.9 jit_solution(13501948108140959160)
XLA Ops:
  0.6 20.4 %shard_map.83 = (s32[4,1440]{1,0:T(4,128)S(1)}, f32[4,4,1440]{2,1,0:T(4,128)S(1)}, f32[4,4,1440]{2,1,0:T(4,128)S(1)}, f32[4,1440]{1,0:T(4,128)S(1)}, f32[4,2048]...) custom-call(f32[4,2048]{1,0:T(4,128)} %rad_hbm.1, s32[1,2048]{1,0:T(1,128)} %bitcast.3, ...), custom_call_target="tpu_custom_call" | custom-call | tf_op jit(solution)/shard_map/pallas_call | solution.py:463
  21.0 0.9 %shard_map.84 = (s32[4,1440]{1,0:T(4,128)}, f32[4,4,1440]{2,1,0:T(4,128)}, f32[4,4,1440]{2,1,0:T(4,128)}, f32[4,1440]{1,0:T(4,128)}, f32[4,2048]{1,0:T(4,128)}) custom-call(s32[4,1440]{1,0:T(4,128)S(1)} %get-tuple-element.13.count_ref, f32[4,4,1440]{2,1,0:T(4,128)S(1)} %get-tuple-element.14.mean_ref, f32[4,4,1440]{2,1,0:T(4,128)S(1)} %get-tuple-element.15.var_ref, ...), custom_call_target="tpu_custom_call" | custom-call | tf_op jit(solution)/shard_map/pallas_call | solution.py:496

commit v8 on v7

--- a/solution.py
+++ b/solution.py
@@ -317,7 +317,7 @@
             result.append(only + pltpu.roll(only, 1, 0))
         return result
 
-    turn = 8
+    turn = 4
     for t in reversed(range(NROW // turn)):
         group = order[turn * t : turn * t + turn]
         (looked,) = look(spread_table, group, t, 1)

time: 22.1 us -> 22.1 us (level)
  no operation moved by 1% of the time
where the time goes in v8:
time: 22.1 us; the launch traced here: 21.9 us
  Pallas kernels  21.3 us (96%)
  between operations  0.64 us (3%)
    pallas_call x1, Pallas kernels, body(): pl.pallas_call(comm_kernel, out_shape=between, in_specs=[hbm] * 4, out_sp...  20.4 us
    pallas_call x1, Pallas kernels, body(): pl.pallas_call(last_kernel, out_shape=outs, in_specs=[vmem] * 8, out_spec...  0.88 us

profile of v8, /device:TPU:1, one launch (start us, length us, event | category | flops | bytes accessed | tf_op | source)
XLA Modules:
  0.0 21.9 jit_solution(8798937430514488121)
XLA Ops:
  0.6 20.4 %shard_map.83 = (s32[4,1440]{1,0:T(4,128)S(1)}, f32[4,4,1440]{2,1,0:T(4,128)S(1)}, f32[4,4,1440]{2,1,0:T(4,128)S(1)}, f32[4,1440]{1,0:T(4,128)S(1)}, f32[4,2048]...) custom-call(f32[4,2048]{1,0:T(4,128)} %rad_hbm.1, s32[1,2048]{1,0:T(1,128)} %bitcast.3, ...), custom_call_target="tpu_custom_call" | custom-call | tf_op jit(solution)/shard_map/pallas_call | solution.py:463
  21.0 0.9 %shard_map.84 = (s32[4,1440]{1,0:T(4,128)}, f32[4,4,1440]{2,1,0:T(4,128)}, f32[4,4,1440]{2,1,0:T(4,128)}, f32[4,1440]{1,0:T(4,128)}, f32[4,2048]{1,0:T(4,128)}) custom-call(s32[4,1440]{1,0:T(4,128)S(1)} %get-tuple-element.13.count_ref, f32[4,4,1440]{2,1,0:T(4,128)S(1)} %get-tuple-element.14.mean_ref, f32[4,4,1440]{2,1,0:T(4,128)S(1)} %get-tuple-element.15.var_ref, ...), custom_call_target="tpu_custom_call" | custom-call | tf_op jit(solution)/shard_map/pallas_call | solution.py:496
